TPU v7x, 32 devices: a whole 2x2x4 slice. The times are simulated.
32 devices in a mesh: dp: 4 (over y, x), ctx: 8 (over z, core).
Axes of the slice: x: 2, y: 2, z: 4, core: 2. Of those that a mesh axis runs over, the one named last changes fastest.
Arguments:
- layer_input: bfloat16 [4, 1024, 7168], P(None, 'ctx', 'dp'), may hold values from -6 to 6
- kv_latent: bfloat16 [4, 1024, 512], P('dp', 'ctx'), may hold values from -8 to 8
- key_rope: bfloat16 [4, 1024, 64], P('dp', 'ctx'), may hold values from -6 to 6
- q_latent: bfloat16 [4, 1024, 8, 512], P('dp', 'ctx'), may hold values from -60 to 60
- q_rope: bfloat16 [4, 1024, 8, 64], P('dp', 'ctx'), may hold values from -3 to 3
- saved_output: bfloat16 [4, 1024, 8, 512], P('dp', 'ctx'), may hold values from -4 to 4
- w_uv: bfloat16 [512, 1024], replicated, may hold values from -0.25 to 0.25
- d_out: bfloat16 [4, 1024, 1024], P('dp', 'ctx'), may hold values from -6 to 6
- blocks: int32 [16], replicated, may hold values from 0 to 15, each once
Outputs:
- d_q_latent: bfloat16 [4, 1024, 8, 512], P('dp', 'ctx')
- d_q_rope: bfloat16 [4, 1024, 8, 64], P('dp', 'ctx')
- d_kv_latent: bfloat16 [4, 1024, 512], P('dp', 'ctx')
- d_key_rope: bfloat16 [4, 1024, 64], P('dp', 'ctx')
- grad_w_down: float32 [7168, 576], P(('dp', 'ctx'))
- grad_w_uv: float32 [512, 1024], P(('dp', 'ctx'))
Inputs may be any that keep to these rules, and one draw needn't show every extreme that they name: A permutation: blocks[k] is the position block of rows k * 64 to (k + 1) * 64 - 1 of every sequence.
All inputs are finite; a program needn't handle non-finite values.
Results may differ from a plain program's by a relative error of at most 0.028.
Values may be sent and summed in bfloat16 or wider, within the bound.
A program may use at most 128 MiB of HBM per device.

v0:
```python
import functools
import math

import jax
import jax.numpy as jnp
from jax import lax
from jax.experimental import pallas as pl
from jax.experimental.pallas import tpu as pltpu
from jax.sharding import PartitionSpec as P

softmax_scale = 1.0 / math.sqrt(192.0)
wide = jnp.float32
low = jnp.bfloat16
MESH = pl.DeviceIdType.MESH
VMEM_LIMIT = 62 * 1024 * 1024


def dot(a, b, ca, cb):
    return lax.dot_general(a, b, (((ca,), (cb,)), ((), ())), preferred_element_type=wide)


def greet(peers):
    barrier = pltpu.get_barrier_semaphore()
    for peer in peers:
        pl.semaphore_signal(barrier, inc=1, device_id=peer, device_id_type=MESH)
    pl.semaphore_wait(barrier, len(peers))


def remote(src, dst, send, recv, peer):
    return pltpu.make_async_remote_copy(
        src_ref=src, dst_ref=dst, send_sem=send, recv_sem=recv, device_id=peer, device_id_type=MESH
    )


def gather_kernel(
    n_dp, n_ctx,
    lat_ref, rope_ref, out_ref, weight_ref, saved_ref,
    keys_ref, grad_ref, delta_ref, value_ref,
    key_ref, spread_ref, parts, landed, key_send, key_recv, pair_send, pair_recv, val_send, val_recv,
):
    dp, ctx = lax.axis_index("dp"), lax.axis_index("ctx")
    n_z = n_ctx // 2
    z, core = ctx // 2, ctx % 2
    tokens, latent = lat_ref.shape
    partner = (dp, z * 2 + (1 - core))
    key_ref[:, :latent] = lat_ref[...]
    key_ref[:, latent:] = rope_ref[...]
    z_peer = lambda k: (dp, lax.rem(z + k, n_z) * 2 + core)
    dp_peer = lambda k: (lax.rem(dp + k, n_dp), ctx)
    greet(
        [partner]
        + [z_peer(k) for k in range(1, n_z)]
        + [dp_peer(k) for k in range(1, n_dp)]
    )

    def rows_of(index):
        return keys_ref.at[pl.ds(pl.multiple_of(index * tokens, tokens), tokens)]

    sends = []
    for k in range(1, n_z):
        copy = remote(key_ref, rows_of(ctx), key_send.at[k], key_recv.at[k], z_peer(k))
        copy.start()
        sends.append(copy)
    pair = remote(key_ref, rows_of(ctx), pair_send.at[0], pair_recv.at[0], partner)
    pair.start()
    keys_ref[pl.ds(pl.multiple_of(ctx * tokens, tokens), tokens), :] = key_ref[...]

    heads = spread_ref.shape[0] // tokens
    values = out_ref.shape[1]
    lane = lax.broadcasted_iota(jnp.int32, (heads, values), 1)
    head = lax.broadcasted_iota(jnp.int32, (heads, values), 0)
    keep = (lane // (values // heads) == head)[None]
    group = min(16, tokens)
    for start in range(0, tokens, group):
        piece = out_ref[start : start + group].astype(wide)
        piece = jnp.broadcast_to(piece[:, None, :], (group, heads, values))
        piece = jnp.where(keep, piece, 0.0).reshape(group * heads, values)
        spread_ref[start * heads : (start + group) * heads, :] = piece.astype(low)

    share = parts.shape[1]
    value = dot(saved_ref[...], spread_ref[...], 0, 0).astype(low)
    for d in range(n_dp):
        parts[d] = value[d * share : (d + 1) * share]
    value_copies = []
    for k in range(1, n_dp):
        copy = remote(
            parts.at[lax.rem(dp + k, n_dp)], landed.at[k], val_send.at[k], val_recv.at[k], dp_peer(k)
        )
        copy.start()
        value_copies.append(copy)

    rows = spread_ref.shape[0]
    tile = min(256, rows)
    for start in range(0, rows, tile):
        grad = dot(spread_ref[start : start + tile], weight_ref[...], 1, 1).astype(low)
        grad_ref[start : start + tile, :] = grad
        prod = grad.astype(wide) * saved_ref[start : start + tile].astype(wide)
        part = prod[:, :128]
        for lane in range(128, prod.shape[1], 128):
            part = part + prod[:, lane : lane + 128]
        delta_ref[:, start : start + tile] = jnp.sum(part.T, axis=0, keepdims=True)

    passes = []
    for k in range(1, n_z):
        owner = lax.rem(z + n_z - k, n_z) * 2 + core
        remote(key_ref, rows_of(owner), key_send.at[k], key_recv.at[k], z_peer(k)).wait_recv()
        copy = remote(rows_of(owner), rows_of(owner), pair_send.at[k], pair_recv.at[k], partner)
        copy.start()
        passes.append(copy)
    total = parts[dp].astype(wide)
    for k in range(1, n_dp):
        value_copies[k - 1].wait_recv()
        total = total + landed[k].astype(wide)
    total = total.astype(low)
    piece = value_ref.shape[1]
    for c in range(n_ctx):
        value_ref[c] = total[c * piece : (c + 1) * piece]
    for k in range(n_z):
        owner = lax.rem(z + n_z - k, n_z) * 2 + (1 - core)
        remote(rows_of(owner), rows_of(owner), pair_send.at[k], pair_recv.at[k], partner).wait_recv()
    for copy in sends + [pair] + passes + value_copies:
        copy.wait_send()


def reduce_kernel(
    n_dp, n_ctx,
    blocks_ref, keys_ref, delta_ref, ql_ref, qr_ref, grad_ref, layer_ref, value_ref,
    dql_ref, dqr_ref, joined_ref, down_ref, uv_ref,
    posk, probs_all, slopes, chip_part, term_out,
    turned, pair_in, pair_sum, z_in, blocks_in, down_out, down_own, down_in, down_sum, down_z, value_in,
    a_send, a_recv, b_send, b_recv, c_send, c_recv, d_send, d_recv, e_send, e_recv, f_send, f_recv,
):
    dp, ctx = lax.axis_index("dp"), lax.axis_index("ctx")
    n_z = n_ctx // 2
    z, core = ctx // 2, ctx % 2
    tokens = joined_ref.shape[0]
    other = 1 - core
    partner = (dp, z * 2 + other)
    chip = lambda k: lax.rem(z + k, n_z)
    z_peer = lambda k: (dp, chip(k) * 2 + core)
    dp_peer = lambda k: (lax.rem(dp + k, n_dp), ctx)
    ctx_peer = lambda k: (dp, lax.rem(ctx + k, n_ctx))
    greet([ctx_peer(k) for k in range(1, n_ctx)] + [dp_peer(k) for k in range(1, n_dp)])
    order = list(range(1, n_z)) + [0]
    pending = []

    def send(src, dst, s, r, peer):
        copy = remote(src, dst, s, r, peer)
        copy.start()
        pending.append(copy)
        return copy

    seq_rows = keys_ref.shape[0]
    rows, latent = ql_ref.shape
    heads = rows // tokens
    half = tokens // 2
    tile = min(256, rows)
    for j in range(seq_rows // half):
        posk[j * half : (j + 1) * half, :] = blocks_ref[j] * half + lax.broadcasted_iota(
            jnp.int32, (half, 1), 0
        )
    low_block, high_block = blocks_ref[2 * ctx], blocks_ref[2 * ctx + 1]

    def score_tile(i, carry):
        span = pl.ds(pl.multiple_of(i * tile, tile), tile)
        token = (i * tile + lax.broadcasted_iota(jnp.int32, (1, tile), 1)) // heads
        posq = jnp.where(token < half, low_block * half + token, high_block * half + token - half)
        key_lat, key_rope = keys_ref[:, :latent], keys_ref[:, latent:]
        scores = dot(key_lat, ql_ref[span, :], 1, 1) + dot(key_rope, qr_ref[span, :], 1, 1)
        scores = jnp.where(posk[...] <= posq, scores * softmax_scale, -jnp.inf)
        expo = jnp.exp(scores - jnp.max(scores, axis=0, keepdims=True))
        probs = expo * (1.0 / jnp.sum(expo, axis=0, keepdims=True))
        grad_prob = dot(key_lat, grad_ref[span, :], 1, 1)
        probs_all[:, span] = probs.astype(low)
        slopes[:, span] = (probs * (grad_prob - delta_ref[:, span])).astype(low)
        return carry

    lax.fori_loop(0, rows // tile, score_tile, 0)

    first, second = {}, {}

    def finish(at):
        k, slot = order[at], at % 2
        first[k].wait_recv()
        added = chip_part[slot, pl.ds(pl.multiple_of(core * tokens, tokens), tokens), :] + pair_in[k].astype(wide)
        if k == 0:
            return added
        pair_sum[k] = added.astype(low)
        second[k] = send(pair_sum.at[k], z_in.at[k], b_send.at[k], b_recv.at[k], z_peer(k))

    for at, k in enumerate(order):
        span = pl.ds(pl.multiple_of(chip(k) * (2 * tokens), 2 * tokens), 2 * tokens)
        slope = slopes[span, :]
        slot = at % 2
        chip_part[slot, :, :latent] = dot(probs_all[span, :], grad_ref[...], 1, 0) + softmax_scale * dot(
            slope, ql_ref[...], 1, 0
        )
        chip_part[slot, :, latent:] = softmax_scale * dot(slope, qr_ref[...], 1, 0)
        term_out[k] = chip_part[slot, pl.ds(pl.multiple_of(other * tokens, tokens), tokens), :].astype(low)
        first[k] = send(term_out.at[k], pair_in.at[k], a_send.at[k], a_recv.at[k], partner)
        if at > 0:
            finish(at - 1)
    mine = finish(n_z - 1)

    def query_tile(i, carry):
        span = pl.ds(pl.multiple_of(i * tile, tile), tile)
        slope = slopes[:, span]
        dql_ref[span, :] = (softmax_scale * dot(slope, keys_ref[:, :latent], 0, 0)).astype(low)
        dqr_ref[span, :] = (softmax_scale * dot(slope, keys_ref[:, latent:], 0, 0)).astype(low)
        return carry

    lax.fori_loop(0, rows // tile, query_tile, 0)
    batch = layer_ref.shape[0]
    for d in range(batch):
        turned[:, d * tokens : (d + 1) * tokens] = layer_ref[d].T
    for k in range(1, n_z):
        second[k].wait_recv()
        mine = mine + z_in[k].astype(wide)
    joined_ref[...] = mine.astype(low)
    blocks_in[dp] = mine.astype(low)

    third = []
    for k in range(1, n_dp):
        third.append(send(joined_ref, blocks_in.at[dp], c_send.at[k], c_recv.at[k], dp_peer(k)))
    values = []
    for k in range(1, n_ctx):
        values.append(
            send(
                value_ref.at[lax.rem(ctx + k, n_ctx)], value_in.at[k], d_send.at[k], d_recv.at[k], ctx_peer(k)
            )
        )
    for copy in third:
        copy.wait_recv()
    every = blocks_in[...].reshape(batch * tokens, blocks_in.shape[2])

    height = down_ref.shape[0]

    def turned_rows(index):
        return turned[pl.ds(pl.multiple_of(index * height, 16), height), :]

    fourth = {}
    for k in order:
        down_out[k] = dot(turned_rows(chip(k) * 2 + other), every, 1, 0).astype(low)
        fourth[k] = send(down_out.at[k], down_in.at[k], e_send.at[k], e_recv.at[k], partner)
    fifth = {}
    own = None
    for k in order:
        part = dot(turned_rows(chip(k) * 2 + core), every, 1, 0)
        fourth[k].wait_recv()
        part = part + down_in[k].astype(wide)
        if k == 0:
            down_own[...] = part
        else:
            down_sum[k] = part.astype(low)
            fifth[k] = send(down_sum.at[k], down_z.at[k], f_send.at[k], f_recv.at[k], z_peer(k))
    value = value_ref[ctx].astype(wide)
    for k in range(1, n_ctx):
        values[k - 1].wait_recv()
        value = value + value_in[k].astype(wide)
    uv_ref[...] = value
    for k in range(1, n_z):
        fifth[k].wait_recv()
        down_own[...] += down_z[k].astype(wide)
    down_ref[...] = down_own[...]
    for copy in pending:
        copy.wait_send()


def body(n_dp, n_ctx, layer_input, kv_latent, key_rope, q_latent, q_rope, saved_output, w_uv, d_out, blocks):
    tokens = kv_latent.shape[1]
    half_rows = tokens // 2
    heads, latent = q_latent.shape[2], q_latent.shape[3]
    rope_width = key_rope.shape[2]
    width = latent + rope_width
    seq_rows = half_rows * blocks.shape[0]
    rows = tokens * heads
    n_z = n_ctx // 2
    values = w_uv.shape[1]
    vmem = pl.BlockSpec(memory_space=pltpu.VMEM)
    dma = lambda n: pltpu.SemaphoreType.DMA((n,))

    saved = saved_output[0].reshape(rows, latent)
    all_keys, grad, delta, value_sum = pl.pallas_call(
        functools.partial(gather_kernel, n_dp, n_ctx),
        out_shape=(
            jax.ShapeDtypeStruct((seq_rows, width), low),
            jax.ShapeDtypeStruct((rows, latent), low),
            jax.ShapeDtypeStruct((1, rows), wide),
            jax.ShapeDtypeStruct((n_ctx, latent // (n_dp * n_ctx), values), low),
        ),
        in_specs=[vmem] * 5,
        out_specs=(vmem,) * 4,
        scratch_shapes=[
            pltpu.VMEM((tokens, width), low),
            pltpu.VMEM((rows, values), low),
            pltpu.VMEM((n_dp, latent // n_dp, values), low),
            pltpu.VMEM((n_dp, latent // n_dp, values), low),
            dma(n_z), dma(n_z), dma(n_z), dma(n_z), dma(n_dp), dma(n_dp),
        ],
        compiler_params=pltpu.CompilerParams(
            collective_id=0, has_side_effects=True, vmem_limit_bytes=VMEM_LIMIT
        ),
        name="gather",
    )(kv_latent[0], key_rope[0], d_out[0], w_uv, saved)

    height = layer_input.shape[2] // n_ctx
    batch = layer_input.shape[0]
    d_lat, d_rope, joined, grad_down, grad_uv = pl.pallas_call(
        functools.partial(reduce_kernel, n_dp, n_ctx),
        out_shape=(
            jax.ShapeDtypeStruct((rows, latent), low),
            jax.ShapeDtypeStruct((rows, rope_width), low),
            jax.ShapeDtypeStruct((tokens, width), low),
            jax.ShapeDtypeStruct((height, width), wide),
            jax.ShapeDtypeStruct((latent // (n_dp * n_ctx), values), wide),
        ),
        in_specs=[pl.BlockSpec(memory_space=pltpu.SMEM)] + [vmem] * 7,
        out_specs=(vmem,) * 5,
        scratch_shapes=[
            pltpu.VMEM((seq_rows, 1), jnp.int32),
            pltpu.VMEM((seq_rows, rows), low),
            pltpu.VMEM((seq_rows, rows), low),
            pltpu.VMEM((2, 2 * tokens, width), wide),
            pltpu.VMEM((n_z, tokens, width), low),
            pltpu.VMEM((layer_input.shape[2], batch * tokens), low),
            pltpu.VMEM((n_z, tokens, width), low),
            pltpu.VMEM((n_z, tokens, width), low),
            pltpu.VMEM((n_z, tokens, width), low),
            pltpu.VMEM((n_dp, tokens, width), low),
            pltpu.VMEM((n_z, height, width), low),
            pltpu.VMEM((height, width), wide),
            pltpu.VMEM((n_z, height, width), low),
            pltpu.VMEM((n_z, height, width), low),
            pltpu.VMEM((n_z, height, width), low),
            pltpu.VMEM((n_ctx, latent // (n_dp * n_ctx), values), low),
            dma(n_z), dma(n_z), dma(n_z), dma(n_z), dma(n_dp), dma(n_dp),
            dma(n_ctx), dma(n_ctx), dma(n_z), dma(n_z), dma(n_z), dma(n_z),
        ],
        compiler_params=pltpu.CompilerParams(
            collective_id=1, has_side_effects=True, vmem_limit_bytes=VMEM_LIMIT
        ),
        name="reduce",
    )(
        blocks, all_keys, delta,
        q_latent[0].reshape(rows, latent), q_rope[0].reshape(rows, rope_width),
        grad, layer_input, value_sum,
    )
    return (
        d_lat.reshape(1, tokens, heads, latent),
        d_rope.reshape(1, tokens, heads, rope_width),
        joined[None, :, :latent],
        joined[None, :, latent:],
        grad_down,
        grad_uv,
    )


def solution(mesh):
    n_dp, n_ctx = mesh.shape["dp"], mesh.shape["ctx"]
    in_specs = (
        P(None, "ctx", "dp"),
        P("dp", "ctx", None),
        P("dp", "ctx", None),
        P("dp", "ctx", None, None),
        P("dp", "ctx", None, None),
        P("dp", "ctx", None, None),
        P(),
        P("dp", "ctx", None),
        P(),
    )
    out_specs = (
        P("dp", "ctx", None, None),
        P("dp", "ctx", None, None),
        P("dp", "ctx", None),
        P("dp", "ctx", None),
        P(("dp", "ctx"), None),
        P(("dp", "ctx"), None),
    )
    return jax.shard_map(
        functools.partial(body, n_dp, n_ctx),
        mesh=mesh, in_specs=in_specs, out_specs=out_specs, check_vma=False,
    )
```

profile of v0, /device:TPU:27, one launch (start us, length us, event | category | flops | bytes accessed | tf_op | source)
XLA Modules:
  0.0 104.0 jit_solution(11402013166499354364)
XLA Ops:
  0.6 1.4 %copy.15 = bf16[1,128,64]{2,1,0:T(8,128)(2,1)} copy(bf16[1,128,64]{1,2,0:T(8,128)(2,1)} %param.11) | data formatting | bytes 32768 | tf_op args[2]
  2.1 1.8 %copy.16 = bf16[1,128,8,64]{3,2,1,0:T(8,128)(2,1)} copy(bf16[1,128,8,64]{1,3,2,0:T(8,128)(2,1)} %param.13) | data formatting | bytes 262144 | tf_op args[4]
  3.8 22.6 %gather.1 = (bf16[1024,576]{1,0:T(8,128)(2,1)}, bf16[1024,512]{1,0:T(8,128)(2,1)}, f32[1,1024]{1,0:T(1,128)}, bf16[8,16,1024]{2,1,0:T(8,128)(2,1)}) custom-call(bf16[128,512]{1,0:T(8,128)(2,1)} %bitcast.19, bf16[128,64]{1,0:T(8,128)(2,1)} %bitcast.18, bf16[128,1024]{1,0:T(8,128)(2,1)} %bitcast.16, bf16[512,1024]{1,0:T(8,128)(2,1)} %weight_ref.1, ...), custom_call_target="tpu_custom_call" | custom-call | tf_op jit(solution)/shard_map/gather/pallas_call | solution.py:283
  26.4 68.9 %reduce.1 = (bf16[1024,512]{1,0:T(8,128)(2,1)}, bf16[1024,64]{1,0:T(8,128)(2,1)}, bf16[128,576]{1,0:T(8,128)(2,1)}, f32[224,576]{1,0:T(8,128)}, f32[16,1024]{1,0:T(8,128)}) custom-call(s32[16]{0:T(128)} %blocks_ref.1, bf16[1024,576]{1,0:T(8,128)(2,1)} %get-tuple-element.15.keys_ref, f32[1,1024]{1,0:T(1,128)} %get-tuple-element.16.delta_ref, ...), custom_call_target="tpu_custom_call" | custom-call | tf_op jit(solution)/shard_map/reduce/pallas_call | solution.py:308
  95.4 0.0 copy-start
  95.4 1.8 %copy.17 = bf16[1,128,8,64]{1,3,2,0:T(8,128)(2,1)} copy(bf16[1,128,8,64]{3,2,1,0:T(8,128)(2,1)} %bitcast.17) | data formatting | bytes 262144
  97.2 0.0 copy-start.1
  97.2 0.8 slice_bitcast_fusion.1
  98.0 1.6 %slice_bitcast_fusion = bf16[1,128,512]{2,1,0:T(8,128)(2,1)} fusion(bf16[128,576]{1,0:T(8,128)(2,1)} %get-tuple-element.21), kind=kLoop, calls=%fused_computation | loop fusion | bytes 262144 | tf_op jit(solution)/shard_map/broadcast_in_dim | solution.py:351
  99.6 0.7 copy.18
  100.3 2.3 %copy.22 = bf16[1,128,8,512]{3,2,1,0:T(8,128)(2,1)} copy(bf16[1,128,8,512]{3,2,1,0:T(8,128)(2,1)} %bitcast.13) | data formatting | bytes 2097152
  102.5 0.0 copy-done
  102.5 0.8 copy.23
  103.4 0.0 copy-done.1
  103.4 0.6 copy.24
Async XLA Ops:
  95.4 7.2 %copy-start = (f32[224,576]{1,0:T(8,128)S(1)}, f32[224,576]{1,0:T(8,128)}, u32[]{:S(2)}) copy-start(f32[224,576]{1,0:T(8,128)} %get-tuple-element.40) | copy-start | bytes 1548292
  97.2 6.1 %copy-start.1 = (f32[16,1024]{1,0:T(8,128)S(1)}, f32[16,1024]{1,0:T(8,128)}, u32[]{:S(2)}) copy-start(f32[16,1024]{1,0:T(8,128)} %get-tuple-element.41) | copy-start | bytes 196612
where the time goes:
time: 104 us
  Pallas kernels  91.5 us (88%)
  local copies, waits for them, and re-layouts  11.8 us (11%)
    pallas_call x1, Pallas kernels, body(): pl.pallas_call(functools.partial(reduce_kernel, n_dp, n_ctx), out_shape=(...  68.9 us
    pallas_call x1, Pallas kernels, body(): pl.pallas_call(functools.partial(gather_kernel, n_dp, n_ctx), out_shape=(...  22.6 us
    unnamed x11, local copies, waits for them, and re-layouts  9.44 us

commit v1 on v0

v1 whole, which is shorter than its diff:
```python
import functools
import math

import jax
import jax.numpy as jnp
from jax import lax
from jax.experimental import pallas as pl
from jax.experimental.pallas import tpu as pltpu
from jax.sharding import PartitionSpec as P

softmax_scale = 1.0 / math.sqrt(192.0)
score_scale = softmax_scale / math.log(2.0)
hidden_score = -1e30
wide = jnp.float32
low = jnp.bfloat16
MESH = pl.DeviceIdType.MESH
VMEM_LIMIT = 58 * 1024 * 1024
HYBRID = False


def dot(a, b, ca, cb):
    return lax.dot_general(a, b, (((ca,), (cb,)), ((), ())), preferred_element_type=wide)


def remote(src, dst, send, recv, peer):
    return pltpu.make_async_remote_copy(
        src_ref=src, dst_ref=dst, send_sem=send, recv_sem=recv, device_id=peer, device_id_type=MESH
    )


def pick(z, values):
    values = [int(v) for v in values]
    if all(v == values[0] for v in values):
        return values[0]
    out = values[0]
    for at, v in enumerate(values[1:], 1):
        out = jnp.where(z == at, v, out)
    return out


def flag(z, values):
    values = [bool(v) for v in values]
    if all(values) or not any(values):
        return values[0]
    return pick(z, values) == 1


def when(condition, action):
    if condition is True:
        action()
    elif condition is not False:
        pl.when(condition)(action)


def otherwise(condition, action):
    if condition is False:
        action()
    elif condition is not True:
        pl.when(jnp.logical_not(condition))(action)


class Line:
    def __init__(self, n):
        self.n, self.hybrid = n, HYBRID and n >= 4
        far = lambda z: sorted([d for d in range(n) if d != z], key=lambda d: (-abs(d - z), d))
        self.near = [sorted([d for d in range(n) if d != z], key=lambda d: (abs(d - z), d)) for z in range(n)]
        self.gather = [[d for d in far(z) if not self.ends(z, d)] + [d for d in far(z) if self.ends(z, d)] for z in range(n)]
        self.reduce = []
        for z in range(n):
            order = far(z)
            relayed = [d for d in order if self.consumes(z, d)]
            self.reduce.append([d for d in order if d not in relayed] + relayed + [z])

    def ends(self, z, d):
        return self.hybrid and {z, d} == {0, self.n - 1}

    def consumes(self, z, d):
        return self.hybrid and (z, d) in ((1, self.n - 1), (self.n - 2, 0))

    def column(self, table, at):
        return [row[at] for row in table]


def main_kernel(
    n_dp, n_ctx,
    blocks_ref, lat_hbm, rope_hbm, ql_hbm, qr_hbm, saved_hbm, weight_hbm, out_hbm, layer_hbm,
    dql_ref, dqr_ref, dlat_ref, drope_ref, down_ref, uv_ref,
    lat_all, rope_all, kr2, ql, qrt, qrf, qr2, qr2t, saved, weight, dout, layer, turned,
    spread, grad, delta, posk, expo, slope, tops, sums, factor,
    val_parts, val_landed, val_total, val_term, val_pair, val_sum, val_in,
    own_a, term_a, pair_a, sum_a, in_a, relay_a, acc_a, msg_a, blocks_a,
    own_b, term_b, pair_b, sum_b, in_b, relay_b, acc_b, msg_b, blocks_b,
    own_c, term_c, pair_c, sum_c, in_c, relay_c, acc_c,
    own_d, term_d, pair_d, sum_d, in_d, relay_d, acc_d,
    rope_lo, rope_hi,
    local_sem, key_send, key_recv, fwd_send, fwd_recv, relay_send,
    val_send, val_recv, vp_send, vp_recv, vz_send, vz_recv,
    pair_send, pair_recv, z_send, z_recv, rl_recv, dp_send, dp_recv,
):
    dp, ctx = lax.axis_index("dp"), lax.axis_index("ctx")
    n_z = n_ctx // 2
    z, core = ctx // 2, ctx % 2
    other = 1 - core
    line = Line(n_z)
    partner = (dp, z * 2 + other)
    chip_peer = lambda c: (dp, c * 2 + core)
    dp_peer = lambda k: (lax.rem(dp + k, n_dp), ctx)
    tokens, latent = lat_hbm.shape
    rope_width = rope_hbm.shape[0]
    rows = ql.shape[0]
    heads = rows // tokens
    half = tokens // 2
    chip_rows = 2 * tokens
    values = dout.shape[1]
    part = latent // 2
    pending = []

    def local(at, src, dst):
        copy = pltpu.make_async_copy(src, dst, local_sem.at[at])
        copy.start()
        return copy

    lat_in = local(0, lat_hbm, lat_all.at[ctx])
    rope_in = local(1, rope_hbm, rope_all.at[ctx])
    out_in = local(2, out_hbm, dout)
    qr_in = local(3, qr_hbm, qrt)
    saved_in = local(4, saved_hbm, saved)
    weight_in = local(5, weight_hbm, weight)
    ql_in = local(6, ql_hbm, ql)
    layer_in = local(7, layer_hbm, layer)

    peers = [partner]
    peers += [chip_peer(lax.rem(z + k, n_z)) for k in range(1, n_z)]
    peers += [dp_peer(k) for k in range(1, n_dp)]
    barrier = pltpu.get_barrier_semaphore()
    for peer in peers:
        pl.semaphore_signal(barrier, inc=1, device_id=peer, device_id_type=MESH)
    for j in range(2 * n_ctx):
        posk[j * half : (j + 1) * half, :] = blocks_ref[j] * half + lax.broadcasted_iota(jnp.int32, (half, 1), 0)
    lat_in.wait()
    rope_in.wait()
    pl.semaphore_wait(barrier, len(peers))

    def key_copies(owner, sends, recvs, send_at, recv_at, peer):
        index = owner * 2 + core
        return [
            remote(lat_all.at[index], lat_all.at[index], sends.at[send_at], recvs.at[recv_at], peer),
            remote(
                rope_all.at[index], rope_all.at[index], sends.at[n_z + send_at], recvs.at[n_z + recv_at], peer
            ),
        ]

    def start_all(copies):
        for copy in copies:
            copy.start()

    def send_waits(copies):
        for copy in copies:
            copy.wait_send()

    def key_recv_wait(owner):
        for copy in key_copies(owner, key_send, key_recv, 0, owner, partner):
            copy.wait_recv()

    for at in range(n_z - 1):
        dest = pick(z, line.column(line.gather, at))
        ok = flag(z, [not line.ends(c, line.gather[c][at]) for c in range(n_z)])
        copies = key_copies(z, key_send, key_recv, at, z, chip_peer(dest))
        when(ok, functools.partial(start_all, copies))
        pending.append((ok, copies))
    copies = key_copies(z, fwd_send, fwd_recv, z, z, partner)
    start_all(copies)
    pending.append((True, copies))

    out_in.wait()
    lane = lax.broadcasted_iota(jnp.int32, (heads, values), 1)
    head = lax.broadcasted_iota(jnp.int32, (heads, values), 0)
    keep = (lane // (values // heads) == head)[None]
    group = min(16, tokens)
    for start in range(0, tokens, group):
        piece = dout[start : start + group].astype(wide)
        piece = jnp.broadcast_to(piece[:, None, :], (group, heads, values))
        piece = jnp.where(keep, piece, 0.0).reshape(group * heads, values)
        spread[start * heads : (start + group) * heads, :] = piece.astype(low)

    qr_in.wait()
    two = 2 * rope_width
    lower = lax.broadcasted_iota(jnp.int32, (tokens, two), 1) < rope_width
    for at in range(heads // 2):
        piece = qrt[2 * at : 2 * at + 2].reshape(two, tokens).astype(wide).T
        qrf[pl.ds(2 * at, tokens, stride=heads), :] = jnp.where(lower, piece, 0.0)
        qrf[pl.ds(2 * at + 1, tokens, stride=heads), :] = jnp.where(lower, 0.0, piece)
    qr2[...] = qrf[...].astype(low)
    qr2t[...] = qrf[...].T.astype(low)

    saved_in.wait()
    weight_in.wait()
    tile = min(256, rows)
    for start in range(0, rows, tile):
        piece = dot(spread[start : start + tile], weight[...], 1, 1).astype(low)
        grad[start : start + tile, :] = piece
        prod = piece.astype(wide) * saved[start : start + tile].astype(wide)
        total = prod[:, :128]
        for at in range(128, prod.shape[1], 128):
            total = total + prod[:, at : at + 128]
        delta[:, start : start + tile] = jnp.sum(total.T, axis=0, keepdims=True)
    ql_in.wait()

    low_block, high_block = blocks_ref[2 * ctx], blocks_ref[2 * ctx + 1]

    def pass_on(owner):
        copies = key_copies(owner, fwd_send, fwd_recv, owner, owner, partner)
        start_all(copies)
        pending.append((True, copies))

    def chunk(owner):
        for copy in key_copies(owner, fwd_send, fwd_recv, 0, owner, partner):
            copy.wait_recv()
        keys = pl.ds(pl.multiple_of(owner * chip_rows, chip_rows), chip_rows)
        for at in range(2):
            piece = rope_all[owner * 2 + at].astype(wide)
            kr2[pl.ds(pl.multiple_of((owner * 2 + at) * tokens, tokens), tokens), :] = (
                jnp.concatenate([piece, piece], axis=0).T.astype(low)
            )

        def score_tile(i, carry):
            if isinstance(i, int):
                span = pl.ds(i * tile, tile)
            else:
                span = pl.ds(pl.multiple_of(i * tile, tile), tile)
            key_lat = lat_all[pl.ds(owner * 2, 2)].reshape(chip_rows, latent)
            scores = dot(key_lat, ql[span, :], 1, 1) + dot(kr2[keys, :], qr2[span, :], 1, 1)
            token = (i * tile + lax.broadcasted_iota(jnp.int32, (1, tile), 1)) // heads
            posq = jnp.where(token < half, low_block * half + token, high_block * half + token - half)
            scores = jnp.where(posk[keys, :] <= posq, scores * score_scale, hidden_score)
            top = jnp.max(scores, axis=0, keepdims=True)
            piece = jnp.exp2(scores - top)
            tops[owner, :, span] = top
            sums[owner, :, span] = jnp.sum(piece, axis=0, keepdims=True)
            expo[keys, span] = piece.astype(low)
            grad_prob = dot(key_lat, grad[span, :], 1, 1)
            slope[keys, span] = (piece * (grad_prob - delta[:, span])).astype(low)
            return carry

        if n_z <= 4:
            for i in range(rows // tile):
                score_tile(i, 0)
        else:
            lax.fori_loop(0, rows // tile, score_tile, 0)

    chunk(z)

    share = val_parts.shape[1]
    value = dot(saved[...], spread[...], 0, 0).astype(low)
    for d in range(n_dp):
        val_parts[d] = value[d * share : (d + 1) * share]
    value_copies = []
    for k in range(1, n_dp):
        copy = remote(
            val_parts.at[lax.rem(dp + k, n_dp)], val_landed.at[k], val_send.at[k], val_recv.at[k], dp_peer(k)
        )
        copy.start()
        value_copies.append(copy)
    pending.append((True, value_copies))

    height = down_ref.shape[0]
    padded = turned.shape[1]
    batch = layer.shape[0]

    def turn():
        layer_in.wait()
        for d in range(batch):
            piece = layer[d].T
            for c in range(n_ctx):
                rows_c = piece[c * height : (c + 1) * height]
                if padded > height:
                    rows_c = jnp.concatenate(
                        [rows_c.astype(wide), jnp.zeros((padded - height, tokens), wide)], axis=0
                    ).astype(low)
                turned[c, :, d * tokens : (d + 1) * tokens] = rows_c

    for at in range(n_z - 1):
        owner = pick(z, line.column(line.near, at))
        key_recv_wait(owner)
        pass_on(owner)
        relay_ok = flag(z, [line.hybrid and (c, line.near[c][at]) in ((1, n_z - 1), (n_z - 2, 0)) for c in range(n_z)])
        if relay_ok is not False:
            end = jnp.where(z == 1, 0, n_z - 1)
            index = owner * 2 + core
            copies = [
                remote(lat_all.at[index], lat_all.at[index], relay_send.at[0], key_recv.at[owner], chip_peer(end)),
                remote(
                    rope_all.at[index], rope_all.at[index], relay_send.at[1], key_recv.at[n_z + owner], chip_peer(end)
                ),
            ]
            when(relay_ok, functools.partial(start_all, copies))
            pending.append((relay_ok, copies))
        if at == n_z - 2:
            turn()
        chunk(owner)

    top = tops[0]
    for c in range(1, n_z):
        top = jnp.maximum(top, tops[c])
    total = jnp.zeros_like(top)
    for c in range(n_z):
        weight_c = jnp.exp2(tops[c] - top)
        factor[c] = weight_c
        total = total + sums[c] * weight_c
    inverse = 1.0 / total
    for c in range(n_z):
        factor[c] = factor[c] * inverse

    def pair_copy(s, at, term, landing):
        return remote(term.at[at], landing.at[at], pair_send.at[s * n_z + at], pair_recv.at[s * n_z + at], partner)

    def relay_copy(s, at, sums_out, relay_in):
        neighbour = jnp.where(z == 0, 1, n_z - 2)
        return remote(sums_out.at[at], relay_in, z_send.at[s * n_z + at], rl_recv.at[s], chip_peer(neighbour))

    def reduce_set(s, compute, own, term, landing, sums_out, z_in, relay_in, acc):
        def finish(at):
            pair_copy(s, at, term, landing).wait_recv()
            added = own[at % 2] + landing[at].astype(wide)
            if at == n_z - 1:
                acc[...] = added
                return
            consumer = flag(z, [line.consumes(c, line.reduce[c][at]) for c in range(n_z)])

            def with_relay():
                relay_copy(s, at, sums_out, relay_in).wait_recv()
                sums_out[at] = (added + relay_in[...].astype(wide)).astype(low)

            def without():
                sums_out[at] = added.astype(low)

            when(consumer, with_relay)
            otherwise(consumer, without)
            dest = pick(z, line.column(line.reduce, at))
            origin = flag(z, [line.ends(c, line.reduce[c][at]) for c in range(n_z)])
            straight = remote(
                sums_out.at[at], z_in.at[z], z_send.at[s * n_z + at], z_recv.at[s * n_z + z], chip_peer(dest)
            )
            if origin is not False:
                when(origin, lambda: relay_copy(s, at, sums_out, relay_in).start())
            otherwise(origin, lambda: straight.start())
            pending.append((True, [straight]))

        for at in range(n_z):
            dest = pick(z, line.column(line.reduce, at))
            compute(at, dest)
            copy = pair_copy(s, at, term, landing)
            copy.start()
            pending.append((True, [copy]))
            if at > 0:
                finish(at - 1)
        finish(n_z - 1)

    def collect(s, sums_out, z_in, acc):
        for at in range(n_z - 1):
            source = pick(z, line.column(line.near, at))
            ok = flag(z, [not line.ends(c, line.near[c][at]) for c in range(n_z)])

            def add():
                remote(
                    sums_out.at[0], z_in.at[source], z_send.at[s * n_z], z_recv.at[s * n_z + source], partner
                ).wait_recv()
                acc[...] += z_in[source].astype(wide)

            when(ok, add)

    def keys_of(c):
        return pl.ds(pl.multiple_of(c * chip_rows, chip_rows), chip_rows)

    def term_first(at, dest):
        keys = keys_of(dest)
        scale = factor[dest]
        expo[keys, :] = (expo[keys, :].astype(wide) * scale).astype(low)
        slope[keys, :] = (slope[keys, :].astype(wide) * (scale * softmax_scale)).astype(low)
        value = dot(expo[keys, :], grad[:, :part], 1, 0) + dot(slope[keys, :], ql[:, :part], 1, 0)
        stage_a[0] = value[:tokens]
        stage_a[1] = value[tokens:]
        own_a[at % 2] = stage_a[core]
        term_a[at] = stage_a[other].astype(low)

    def term_second(at, dest):
        keys = keys_of(dest)
        value = dot(expo[keys, :], grad[:, part:], 1, 0) + dot(slope[keys, :], ql[:, part:], 1, 0)
        rope = dot(qr2t[...], slope[keys, :], 1, 1)
        rope = rope[:rope_width] + rope[rope_width:]
        quarter = rope_width // 2
        for c in range(2):
            stage_b[c, :tokens, :] = value[c * tokens : (c + 1) * tokens]
            mine = rope[:, c * tokens : (c + 1) * tokens]
            stage_b[c, tokens:, :] = jnp.concatenate([mine[:quarter], mine[quarter:]], axis=1)
        own_b[at % 2] = stage_b[core]
        term_b[at] = stage_b[other].astype(low)

    stage_a, stage_b = own_a.at[pl.ds(2, 2)], own_b.at[pl.ds(2, 2)]
    reduce_set(0, term_first, own_a, term_a, pair_a, sum_a, in_a, relay_a, acc_a)
    reduce_set(1, term_second, own_b, term_b, pair_b, sum_b, in_b, relay_b, acc_b)

    total = val_parts[dp].astype(wide)
    for k in range(1, n_dp):
        value_copies[k - 1].wait_recv()
        total = total + val_landed[k].astype(wide)
    piece = val_total.shape[1]
    for c in range(n_ctx):
        val_total[c] = total[c * piece : (c + 1) * piece]
    value_pairs = []
    for k in range(n_z):
        dest = lax.rem(z + k, n_z)
        val_term[k] = val_total[dest * 2 + other].astype(low)
        copy = remote(val_term.at[k], val_pair.at[k], vp_send.at[k], vp_recv.at[k], partner)
        copy.start()
        value_pairs.append(copy)
    pending.append((True, value_pairs))

    def query_tile(i, carry):
        if isinstance(i, int):
            span = pl.ds(i * tile, tile)
        else:
            span = pl.ds(pl.multiple_of(i * tile, tile), tile)
        piece = slope[:, span]
        all_lat = lat_all[...].reshape(n_ctx * tokens, latent)
        dql_ref[span, :] = dot(piece, all_lat, 0, 0).astype(low)
        qrf[span, :] = dot(piece, kr2[...], 0, 0)
        return carry

    lax.fori_loop(0, rows // tile, query_tile, 0)
    for at in range(heads // 2):
        even = qrf[pl.ds(2 * at, tokens, stride=heads), :]
        odd = qrf[pl.ds(2 * at + 1, tokens, stride=heads), :]
        piece = jnp.where(lower, even, odd).T.astype(low)
        dqr_ref[2 * at] = piece[:rope_width]
        dqr_ref[2 * at + 1] = piece[rope_width:]

    value_sends = []
    for k in list(range(1, n_z)) + [0]:
        value_pairs[k].wait_recv()
        dest = lax.rem(z + k, n_z)
        added = val_total[dest * 2 + core] + val_pair[k].astype(wide)
        if k == 0:
            uv_ref[...] = added
        else:
            val_sum[k] = added.astype(low)
            copy = remote(val_sum.at[k], val_in.at[k], vz_send.at[k], vz_recv.at[k], chip_peer(dest))
            copy.start()
            value_sends.append(copy)
    pending.append((True, value_sends))

    def spread_dp(s, acc, msg, landing):
        msg[...] = acc[...].astype(low)
        landing[dp] = msg[...]
        copies = []
        for k in range(1, n_dp):
            copy = remote(
                msg, landing.at[dp], dp_send.at[s * n_dp + k], dp_recv.at[s * n_dp + k], dp_peer(k)
            )
            copy.start()
            copies.append(copy)
        pending.append((True, copies))
        return copies

    collect(0, sum_a, in_a, acc_a)
    first = spread_dp(0, acc_a, msg_a, blocks_a)
    dlat_ref[:, :part] = msg_a[...]
    collect(1, sum_b, in_b, acc_b)
    second = spread_dp(1, acc_b, msg_b, blocks_b)
    dlat_ref[:, part:] = msg_b[:tokens, :]
    quarter = rope_width // 2
    drope_ref[:quarter, :] = msg_b[tokens:, :tokens]
    drope_ref[quarter:, :] = msg_b[tokens:, tokens:]

    for copy in first:
        copy.wait_recv()

    def down_first(at, dest):
        every = blocks_a[...].reshape(batch * tokens, part)
        term_c[at] = dot(turned[dest * 2 + other], every, 1, 0).astype(low)
        own_c[at % 2] = dot(turned[dest * 2 + core], every, 1, 0)

    reduce_set(2, down_first, own_c, term_c, pair_c, sum_c, in_c, relay_c, acc_c)

    for copy in second:
        copy.wait_recv()
    packed = height % 32 == 0
    for b in range(batch):
        piece = blocks_b[b, tokens:, :]
        cols = slice(b * tokens, (b + 1) * tokens)
        for at in range(2):
            rope_lo[at * quarter : (at + 1) * quarter, cols] = piece[:, at * tokens : (at + 1) * tokens]
            rope_hi[rope_width + at * quarter : rope_width + (at + 1) * quarter, cols] = piece[
                :, at * tokens : (at + 1) * tokens
            ]
    rope_lo[rope_width:, :] = jnp.zeros((rope_width, batch * tokens), low)
    rope_hi[:rope_width, :] = jnp.zeros((rope_width, batch * tokens), low)

    def down_piece(index):
        every = blocks_b[:, :tokens, :].reshape(batch * tokens, part)
        lat = dot(turned[index], every, 1, 0)
        if packed:
            rope = dot(turned[index, : height // 2], rope_lo[...], 1, 1)
            rope = rope + dot(turned[index, height // 2 :], rope_hi[...], 1, 1)
            rope = jnp.concatenate([rope[: height // 4], rope[height // 4 :]], axis=1)
        else:
            rope = dot(turned[index], rope_lo[...], 1, 1)
            rope = jnp.concatenate([rope, jnp.zeros((padded, part - two), wide)], axis=1)
        return lat, rope

    def down_second(at, dest):
        lat, rope = down_piece(dest * 2 + other)
        term_d[at, :padded, :] = lat.astype(low)
        term_d[at, padded:, :] = rope.astype(low)
        lat, rope = down_piece(dest * 2 + core)
        own_d[at % 2, :padded, :] = lat
        own_d[at % 2, padded:, :] = rope

    reduce_set(3, down_second, own_d, term_d, pair_d, sum_d, in_d, relay_d, acc_d)
    for k in range(1, n_z):
        value_sends[k - 1].wait_recv()
        uv_ref[...] += val_in[k].astype(wide)
    collect(2, sum_c, in_c, acc_c)
    down_ref[:, :part] = acc_c[:height, :]
    collect(3, sum_d, in_d, acc_d)
    down_ref[:, part:latent] = acc_d[:height, :]
    if packed:
        rope = acc_d[padded:, :]
        rope = jnp.concatenate([rope[:, :two], rope[:, two:]], axis=0)
        down_ref[: height // 2, latent:] = rope[:, :rope_width]
        down_ref[height // 2 :, latent:] = rope[:, rope_width:]
    else:
        down_ref[:, latent:] = acc_d[padded : padded + height, :rope_width]

    for ok, copies in pending:
        when(ok, functools.partial(send_waits, copies))


def store_kernel(n, *refs):
    sem = refs[2 * n]
    copies = [pltpu.make_async_copy(refs[at], refs[n + at], sem.at[at]) for at in range(n)]
    for copy in copies:
        copy.start()
    for copy in copies:
        copy.wait()


def body(n_dp, n_ctx, layer_input, kv_latent, key_rope, q_latent, q_rope, saved_output, w_uv, d_out, blocks):
    tokens = kv_latent.shape[1]
    heads, latent = q_latent.shape[2], q_latent.shape[3]
    rope_width = key_rope.shape[2]
    rows = tokens * heads
    seq_rows = tokens * n_ctx
    n_z = n_ctx // 2
    values = w_uv.shape[1]
    batch, _, width = layer_input.shape
    height = width // n_ctx
    padded = -(-height // 16) * 16
    extra = height // 4 if height % 32 == 0 else padded
    share = latent // (n_dp * n_ctx)
    part = latent // 2
    two = 2 * rope_width
    vmem = pl.BlockSpec(memory_space=pltpu.VMEM)
    hbm = pl.BlockSpec(memory_space=pltpu.HBM)
    dma = lambda n: pltpu.SemaphoreType.DMA((n,))

    def stage(count, fill, landed):
        half = lambda *dims: pltpu.VMEM((*dims, fill, part), low)
        out = [
            pltpu.VMEM((count, fill, part), wide), half(n_z), half(n_z), half(n_z), half(n_z), half(),
            pltpu.VMEM((fill, part), wide),
        ]
        return out + ([half(), half(batch)] if landed else [])

    outs = (
        ((rows, latent), low),
        ((heads, rope_width, tokens), low),
        ((tokens, latent), low),
        ((rope_width, tokens), low),
        ((height, latent + rope_width), wide),
        ((share, values), wide),
    )
    found = pl.pallas_call(
        functools.partial(main_kernel, n_dp, n_ctx),
        out_shape=tuple(pltpu.VMEM(shape, kind) for shape, kind in outs),
        in_specs=[pl.BlockSpec(memory_space=pltpu.SMEM)] + [hbm] * 8,
        out_specs=(vmem,) * 6,
        scratch_shapes=[
            pltpu.VMEM((n_ctx, tokens, latent), low),
            pltpu.VMEM((n_ctx, rope_width, tokens), low),
            pltpu.VMEM((seq_rows, two), low),
            pltpu.VMEM((rows, latent), low),
            pltpu.VMEM((heads, rope_width, tokens), low),
            pltpu.VMEM((rows, two), wide),
            pltpu.VMEM((rows, two), low),
            pltpu.VMEM((two, rows), low),
            pltpu.VMEM((rows, latent), low),
            pltpu.VMEM((latent, values), low),
            pltpu.VMEM((tokens, values), low),
            pltpu.VMEM(layer_input.shape, low),
            pltpu.VMEM((n_ctx, padded, batch * tokens), low),
            pltpu.VMEM((rows, values), low),
            pltpu.VMEM((rows, latent), low),
            pltpu.VMEM((1, rows), wide),
            pltpu.VMEM((seq_rows, 1), jnp.int32),
            pltpu.VMEM((seq_rows, rows), low),
            pltpu.VMEM((seq_rows, rows), low),
            pltpu.VMEM((n_z, 1, rows), wide),
            pltpu.VMEM((n_z, 1, rows), wide),
            pltpu.VMEM((n_z, 1, rows), wide),
            pltpu.VMEM((n_dp, latent // n_dp, values), low),
            pltpu.VMEM((n_dp, latent // n_dp, values), low),
            pltpu.VMEM((n_ctx, share, values), wide),
            pltpu.VMEM((n_z, share, values), low),
            pltpu.VMEM((n_z, share, values), low),
            pltpu.VMEM((n_z, share, values), low),
            pltpu.VMEM((n_z, share, values), low),
            *stage(4, tokens, True),
            *stage(4, tokens + rope_width // 2, True),
            *stage(2, padded, False),
            *stage(2, padded + extra, False),
            pltpu.VMEM((two, batch * tokens), low),
            pltpu.VMEM((two, batch * tokens), low),
            dma(8), dma(2 * n_z), dma(2 * n_z), dma(2 * n_z), dma(2 * n_z), dma(2),
            dma(n_dp), dma(n_dp), dma(n_z), dma(n_z), dma(n_z), dma(n_z),
            dma(4 * n_z), dma(4 * n_z), dma(4 * n_z), dma(4 * n_z), dma(4), dma(2 * n_dp), dma(2 * n_dp),
        ],
        compiler_params=pltpu.CompilerParams(
            collective_id=0, has_side_effects=True, vmem_limit_bytes=VMEM_LIMIT
        ),
        name="main",
    )(
        blocks, kv_latent[0], key_rope[0].T,
        q_latent[0].reshape(rows, latent), jnp.transpose(q_rope[0], (1, 2, 0)),
        saved_output[0].reshape(rows, latent), w_uv, d_out[0], layer_input,
    )
    d_lat, d_rope, k_lat, k_rope, grad_down, grad_uv = pl.pallas_call(
        functools.partial(store_kernel, len(outs)),
        out_shape=tuple(jax.ShapeDtypeStruct(shape, kind) for shape, kind in outs),
        in_specs=[vmem] * len(outs),
        out_specs=(hbm,) * len(outs),
        scratch_shapes=[dma(len(outs))],
        compiler_params=pltpu.CompilerParams(vmem_limit_bytes=4 * 1024 * 1024),
        name="store",
    )(*found)
    return (
        d_lat.reshape(1, tokens, heads, latent),
        jnp.transpose(d_rope, (2, 0, 1))[None],
        k_lat[None],
        k_rope.T[None],
        grad_down,
        grad_uv,
    )


def solution(mesh):
    n_dp, n_ctx = mesh.shape["dp"], mesh.shape["ctx"]
    in_specs = (
        P(None, "ctx", "dp"),
        P("dp", "ctx", None),
        P("dp", "ctx", None),
        P("dp", "ctx", None, None),
        P("dp", "ctx", None, None),
        P("dp", "ctx", None, None),
        P(),
        P("dp", "ctx", None),
        P(),
    )
    out_specs = (
        P("dp", "ctx", None, None),
        P("dp", "ctx", None, None),
        P("dp", "ctx", None),
        P("dp", "ctx", None),
        P(("dp", "ctx"), None),
        P(("dp", "ctx"), None),
    )
    return jax.shard_map(
        functools.partial(body, n_dp, n_ctx),
        mesh=mesh, in_specs=in_specs, out_specs=out_specs, check_vma=False,
    )
```

time: 104 us -> 68.6 us (0.66)
  the two profiles are of different devices: /device:TPU:27 before, /device:TPU:0 now
where the time goes in v1:
time: 68.6 us; the launch traced here: 67.6 us
  Pallas kernels  66.8 us (97%)
  between operations  0.8 us (1%)
    pallas_call x1, Pallas kernels, body(): pl.pallas_call(functools.partial(main_kernel, n_dp, n_ctx), out_shape=tup...  65.5 us

profile of v1, /device:TPU:0, one launch (start us, length us, event | category | flops | bytes accessed | tf_op | source)
XLA Modules:
  0.0 67.6 jit_solution(7148479548476877188)
XLA Ops:
  0.6 65.5 %main.1 = (bf16[1024,512]{1,0:T(8,128)(2,1)S(1)}, bf16[8,64,128]{2,1,0:T(8,128)(2,1)S(1)}, bf16[128,512]{1,0:T(8,128)(2,1)S(1)}, bf16[64,128]{1,0:T(8,128)(2,1)S...) custom-call(s32[16]{0:T(128)} %blocks_ref.1, bf16[128,512]{1,0:T(8,128)(2,1)} %bitcast.21, bf16[64,128]{1,0:T(8,128)(2,1)} %bitcast.23, ...), custom_call_target="tpu_custom_call" | custom-call | tf_op jit(solution)/shard_map/main/pallas_call | solution.py:583
  66.1 1.3 %store.1 = (bf16[1024,512]{1,0:T(8,128)(2,1)}, bf16[8,64,128]{2,1,0:T(8,128)(2,1)}, bf16[128,512]{1,0:T(8,128)(2,1)}, bf16[64,128]{1,0:T(8,128)(2,1)}, f32[224,576]{1,0:T(8,128)}, /*index=5*/f32[16,1024]{1,0:T(8,128)}) custom-call(bf16[1024,512]{1,0:T(8,128)(2,1)S(1)} %get-tuple-element.18.refs_0_, bf16[8,64,128]{2,1,0:T(8,128)(2,1)S(1)} %get-tuple-element.19.refs_1_, ...), custom_call_target="tpu_custom_call" | custom-call | tf_op jit(solution)/shard_map/store/pallas_call | solution.py:637

commit v2 on v1

--- a/solution.py
+++ b/solution.py
@@ -15,7 +15,7 @@
 low = jnp.bfloat16
 MESH = pl.DeviceIdType.MESH
 VMEM_LIMIT = 58 * 1024 * 1024
-HYBRID = False
+HYBRID = True
 
 
 def dot(a, b, ca, cb):
@@ -64,6 +64,8 @@
         self.n, self.hybrid = n, HYBRID and n >= 4
         far = lambda z: sorted([d for d in range(n) if d != z], key=lambda d: (-abs(d - z), d))
         self.near = [sorted([d for d in range(n) if d != z], key=lambda d: (abs(d - z), d)) for z in range(n)]
+        first = lambda z: [d for d in self.near[z] if self.forwards(z, d)]
+        self.arrive = [first(z) + [d for d in self.near[z] if d not in first(z)] for z in range(n)]
         self.gather = [[d for d in far(z) if not self.ends(z, d)] + [d for d in far(z) if self.ends(z, d)] for z in range(n)]
         self.reduce = []
         for z in range(n):
@@ -76,6 +78,9 @@
 
     def consumes(self, z, d):
         return self.hybrid and (z, d) in ((1, self.n - 1), (self.n - 2, 0))
+
+    def forwards(self, z, owner):
+        return self.hybrid and (z, owner) in ((1, self.n - 1), (self.n - 2, 0))
 
     def column(self, table, at):
         return [row[at] for row in table]
@@ -88,14 +93,12 @@
     lat_all, rope_all, kr2, ql, qrt, qrf, qr2, qr2t, saved, weight, dout, layer, turned,
     spread, grad, delta, posk, expo, slope, tops, sums, factor,
     val_parts, val_landed, val_total, val_term, val_pair, val_sum, val_in,
-    own_a, term_a, pair_a, sum_a, in_a, relay_a, acc_a, msg_a, blocks_a,
-    own_b, term_b, pair_b, sum_b, in_b, relay_b, acc_b, msg_b, blocks_b,
-    own_c, term_c, pair_c, sum_c, in_c, relay_c, acc_c,
+    key_stage, own_k, term_k, pair_k, sum_k, in_k, relay_k, acc_k, message, landed,
     own_d, term_d, pair_d, sum_d, in_d, relay_d, acc_d,
     rope_lo, rope_hi,
     local_sem, key_send, key_recv, fwd_send, fwd_recv, relay_send,
     val_send, val_recv, vp_send, vp_recv, vz_send, vz_recv,
-    pair_send, pair_recv, z_send, z_recv, rl_recv, dp_send, dp_recv,
+    kp_send, kp_recv, kz_send, kz_recv, kr_recv, gp_send, gp_recv, gz_send, gz_recv, gr_recv, dp_send, dp_recv,
 ):
     dp, ctx = lax.axis_index("dp"), lax.axis_index("ctx")
     n_z = n_ctx // 2
@@ -112,7 +115,8 @@
     half = tokens // 2
     chip_rows = 2 * tokens
     values = dout.shape[1]
-    part = latent // 2
+    pieces = 4
+    lanes = latent // pieces
     pending = []
 
     def local(at, src, dst):
@@ -143,11 +147,10 @@
 
     def key_copies(owner, sends, recvs, send_at, recv_at, peer):
         index = owner * 2 + core
+        refs = [lat_all.at[index, pl.ds(0, half)], lat_all.at[index, pl.ds(half, half)], rope_all.at[index]]
         return [
-            remote(lat_all.at[index], lat_all.at[index], sends.at[send_at], recvs.at[recv_at], peer),
-            remote(
-                rope_all.at[index], rope_all.at[index], sends.at[n_z + send_at], recvs.at[n_z + recv_at], peer
-            ),
+            remote(ref, ref, sends.at[n * n_z + send_at], recvs.at[n * n_z + recv_at], peer)
+            for n, ref in enumerate(refs)
         ]
 
     def start_all(copies):
@@ -157,10 +160,6 @@
     def send_waits(copies):
         for copy in copies:
             copy.wait_send()
-
-    def key_recv_wait(owner):
-        for copy in key_copies(owner, key_send, key_recv, 0, owner, partner):
-            copy.wait_recv()
 
     for at in range(n_z - 1):
         dest = pick(z, line.column(line.gather, at))
@@ -194,6 +193,19 @@
     qr2t[...] = qrf[...].T.astype(low)
 
     saved_in.wait()
+    share = val_parts.shape[1]
+    value = dot(saved[...], spread[...], 0, 0).astype(low)
+    for d in range(n_dp):
+        val_parts[d] = value[d * share : (d + 1) * share]
+    value_copies = []
+    for k in range(1, n_dp):
+        copy = remote(
+            val_parts.at[lax.rem(dp + k, n_dp)], val_landed.at[k], val_send.at[k], val_recv.at[k], dp_peer(k)
+        )
+        copy.start()
+        value_copies.append(copy)
+    pending.append((True, value_copies))
+
     weight_in.wait()
     tile = min(256, rows)
     for start in range(0, rows, tile):
@@ -250,19 +262,6 @@
 
     chunk(z)
 
-    share = val_parts.shape[1]
-    value = dot(saved[...], spread[...], 0, 0).astype(low)
-    for d in range(n_dp):
-        val_parts[d] = value[d * share : (d + 1) * share]
-    value_copies = []
-    for k in range(1, n_dp):
-        copy = remote(
-            val_parts.at[lax.rem(dp + k, n_dp)], val_landed.at[k], val_send.at[k], val_recv.at[k], dp_peer(k)
-        )
-        copy.start()
-        value_copies.append(copy)
-    pending.append((True, value_copies))
-
     height = down_ref.shape[0]
     padded = turned.shape[1]
     batch = layer.shape[0]
@@ -279,25 +278,54 @@
                     ).astype(low)
                 turned[c, :, d * tokens : (d + 1) * tokens] = rows_c
 
+    value_pairs, value_sends = [], []
+
+    def pair_values():
+        total = val_parts[dp].astype(wide)
+        for k in range(1, n_dp):
+            value_copies[k - 1].wait_recv()
+            total = total + val_landed[k].astype(wide)
+        piece = val_total.shape[1]
+        for c in range(n_ctx):
+            val_total[c] = total[c * piece : (c + 1) * piece]
+        for k in range(n_z):
+            dest = lax.rem(z + k, n_z)
+            val_term[k] = val_total[dest * 2 + other].astype(low)
+            copy = remote(val_term.at[k], val_pair.at[k], vp_send.at[k], vp_recv.at[k], partner)
+            copy.start()
+            value_pairs.append(copy)
+        pending.append((True, value_pairs))
+
+    def start_values():
+        for k in list(range(1, n_z)) + [0]:
+            value_pairs[k].wait_recv()
+            dest = lax.rem(z + k, n_z)
+            added = val_total[dest * 2 + core] + val_pair[k].astype(wide)
+            if k == 0:
+                uv_ref[...] = added
+            else:
+                val_sum[k] = added.astype(low)
+                copy = remote(val_sum.at[k], val_in.at[k], vz_send.at[k], vz_recv.at[k], chip_peer(dest))
+                copy.start()
+                value_sends.append(copy)
+        pending.append((True, value_sends))
+
     for at in range(n_z - 1):
-        owner = pick(z, line.column(line.near, at))
-        key_recv_wait(owner)
-        pass_on(owner)
-        relay_ok = flag(z, [line.hybrid and (c, line.near[c][at]) in ((1, n_z - 1), (n_z - 2, 0)) for c in range(n_z)])
+        owner = pick(z, line.column(line.arrive, at))
+        relay_ok = flag(z, [line.forwards(c, line.arrive[c][at]) for c in range(n_z)])
+        copies = []
         if relay_ok is not False:
             end = jnp.where(z == 1, 0, n_z - 1)
-            index = owner * 2 + core
-            copies = [
-                remote(lat_all.at[index], lat_all.at[index], relay_send.at[0], key_recv.at[owner], chip_peer(end)),
-                remote(
-                    rope_all.at[index], rope_all.at[index], relay_send.at[1], key_recv.at[n_z + owner], chip_peer(end)
-                ),
-            ]
-            when(relay_ok, functools.partial(start_all, copies))
+            copies = key_copies(owner, relay_send, key_recv, 0, owner, chip_peer(end))
             pending.append((relay_ok, copies))
-        if at == n_z - 2:
+        for n, copy in enumerate(key_copies(owner, key_send, key_recv, 0, owner, partner)):
+            copy.wait_recv()
+            if copies:
+                when(relay_ok, copies[n].start)
+        pass_on(owner)
+        chunk(owner)
+        if at == max(n_z - 3, 0):
             turn()
-        chunk(owner)
 
     top = tops[0]
     for c in range(1, n_z):
@@ -311,226 +339,253 @@
     for c in range(n_z):
         factor[c] = factor[c] * inverse
 
-    def pair_copy(s, at, term, landing):
-        return remote(term.at[at], landing.at[at], pair_send.at[s * n_z + at], pair_recv.at[s * n_z + at], partner)
-
-    def relay_copy(s, at, sums_out, relay_in):
-        neighbour = jnp.where(z == 0, 1, n_z - 2)
-        return remote(sums_out.at[at], relay_in, z_send.at[s * n_z + at], rl_recv.at[s], chip_peer(neighbour))
-
-    def reduce_set(s, compute, own, term, landing, sums_out, z_in, relay_in, acc):
-        def finish(at):
-            pair_copy(s, at, term, landing).wait_recv()
-            added = own[at % 2] + landing[at].astype(wide)
-            if at == n_z - 1:
-                acc[...] = added
-                return
-            consumer = flag(z, [line.consumes(c, line.reduce[c][at]) for c in range(n_z)])
-
-            def with_relay():
-                relay_copy(s, at, sums_out, relay_in).wait_recv()
-                sums_out[at] = (added + relay_in[...].astype(wide)).astype(low)
-
-            def without():
-                sums_out[at] = added.astype(low)
-
-            when(consumer, with_relay)
-            otherwise(consumer, without)
-            dest = pick(z, line.column(line.reduce, at))
-            origin = flag(z, [line.ends(c, line.reduce[c][at]) for c in range(n_z)])
-            straight = remote(
-                sums_out.at[at], z_in.at[z], z_send.at[s * n_z + at], z_recv.at[s * n_z + z], chip_peer(dest)
+    lag, slots = 2, 4
+    neighbour = jnp.where(z == 0, 1, n_z - 2)
+
+    class Reduce:
+        def __init__(self, spans, own, term, landing, total, inbox, relay, acc, sems):
+            self.spans = spans
+            self.own, self.term, self.landing, self.total = own, term, landing, total
+            self.inbox, self.relayed, self.acc = inbox, relay, acc
+            self.pair_send, self.pair_recv, self.send, self.recv, self.relay_recv = sems
+
+        def dest(self, at):
+            return pick(z, line.column(line.reduce, at))
+
+        def pair(self, at, span, sem):
+            return remote(
+                self.term.at[at, span], self.landing.at[at, span], self.pair_send.at[sem], self.pair_recv.at[sem], partner
             )
-            if origin is not False:
-                when(origin, lambda: relay_copy(s, at, sums_out, relay_in).start())
-            otherwise(origin, lambda: straight.start())
-            pending.append((True, [straight]))
-
-        for at in range(n_z):
-            dest = pick(z, line.column(line.reduce, at))
-            compute(at, dest)
-            copy = pair_copy(s, at, term, landing)
+
+        def straight(self, p, at, source=None):
+            sem = p * n_z
+            source = z if source is None else source
+            return remote(
+                self.total.at[at, self.spans[p]], self.inbox.at[source, self.spans[p]],
+                self.send.at[sem + at], self.recv.at[sem + source], chip_peer(self.dest(at)),
+            )
+
+        def aside(self, p, at):
+            return remote(
+                self.total.at[at, self.spans[p]], self.relayed.at[self.spans[p]],
+                self.send.at[p * n_z + at], self.relay_recv.at[p], chip_peer(neighbour),
+            )
+
+        def consumer(self, at):
+            return flag(z, [line.consumes(c, line.reduce[c][at]) for c in range(n_z)])
+
+        def both(self, at, span):
+            return self.own[at % slots, span] + self.landing[at, span].astype(wide)
+
+        def begin(self, at, span, sem):
+            copy = self.pair(at, span, sem)
             copy.start()
             pending.append((True, [copy]))
-            if at > 0:
-                finish(at - 1)
-        finish(n_z - 1)
-
-    def collect(s, sums_out, z_in, acc):
-        for at in range(n_z - 1):
-            source = pick(z, line.column(line.near, at))
-            ok = flag(z, [not line.ends(c, line.near[c][at]) for c in range(n_z)])
-
-            def add():
-                remote(
-                    sums_out.at[0], z_in.at[source], z_send.at[s * n_z], z_recv.at[s * n_z + source], partner
-                ).wait_recv()
-                acc[...] += z_in[source].astype(wide)
-
-            when(ok, add)
-
-    def keys_of(c):
-        return pl.ds(pl.multiple_of(c * chip_rows, chip_rows), chip_rows)
-
-    def term_first(at, dest):
-        keys = keys_of(dest)
+
+        def finish(self, at, span, sem):
+            self.pair(at, span, sem).wait_recv()
+            if at == n_z - 1:
+                self.acc[span] = self.both(at, span)
+            else:
+                self.total[at, span] = self.both(at, span).astype(low)
+
+        def push(self, p, at):
+            if at == n_z - 1:
+                return
+            origin = flag(z, [line.ends(c, line.reduce[c][at]) for c in range(n_z)])
+
+            def out():
+                if origin is not False:
+                    when(origin, self.aside(p, at).start)
+                otherwise(origin, self.straight(p, at).start)
+
+            otherwise(self.consumer(at), out)
+            pending.append((True, [self.straight(p, at)]))
+
+        def relay(self, p):
+            span = self.spans[p]
+            for at in range(n_z - 1):
+
+                def out():
+                    self.aside(p, at).wait_recv()
+                    self.total[at, span] = (self.both(at, span) + self.relayed[span].astype(wide)).astype(low)
+                    self.straight(p, at).start()
+
+                when(self.consumer(at), out)
+
+        def collect(self, p):
+            span = self.spans[p]
+            for at in range(n_z - 1):
+                source = pick(z, line.column(line.near, at))
+                ok = flag(z, [not line.ends(c, line.near[c][at]) for c in range(n_z)])
+
+                def add():
+                    self.straight(p, 0, source).wait_recv()
+                    self.acc[span] += self.inbox[source, span].astype(wide)
+
+                when(ok, add)
+
+    def spans_of(size, tail):
+        return [pl.ds(p * size, size + (tail if p == pieces - 1 else 0)) for p in range(pieces)]
+
+    key_fill = pieces * tokens + rope_width
+    key_all = pl.ds(0, key_fill)
+    key_set = Reduce(
+        spans_of(tokens, rope_width), own_k, term_k, pair_k, sum_k, in_k, relay_k, acc_k,
+        (kp_send, kp_recv, kz_send, kz_recv, kr_recv),
+    )
+
+    def key_terms(at):
+        dest = key_set.dest(at)
+        keys = pl.ds(pl.multiple_of(dest * chip_rows, chip_rows), chip_rows)
         scale = factor[dest]
         expo[keys, :] = (expo[keys, :].astype(wide) * scale).astype(low)
         slope[keys, :] = (slope[keys, :].astype(wide) * (scale * softmax_scale)).astype(low)
-        value = dot(expo[keys, :], grad[:, :part], 1, 0) + dot(slope[keys, :], ql[:, :part], 1, 0)
-        stage_a[0] = value[:tokens]
-        stage_a[1] = value[tokens:]
-        own_a[at % 2] = stage_a[core]
-        term_a[at] = stage_a[other].astype(low)
-
-    def term_second(at, dest):
-        keys = keys_of(dest)
-        value = dot(expo[keys, :], grad[:, part:], 1, 0) + dot(slope[keys, :], ql[:, part:], 1, 0)
+        value = dot(expo[keys, :], grad[...], 1, 0) + dot(slope[keys, :], ql[...], 1, 0)
         rope = dot(qr2t[...], slope[keys, :], 1, 1)
         rope = rope[:rope_width] + rope[rope_width:]
-        quarter = rope_width // 2
         for c in range(2):
-            stage_b[c, :tokens, :] = value[c * tokens : (c + 1) * tokens]
-            mine = rope[:, c * tokens : (c + 1) * tokens]
-            stage_b[c, tokens:, :] = jnp.concatenate([mine[:quarter], mine[quarter:]], axis=1)
-        own_b[at % 2] = stage_b[core]
-        term_b[at] = stage_b[other].astype(low)
-
-    stage_a, stage_b = own_a.at[pl.ds(2, 2)], own_b.at[pl.ds(2, 2)]
-    reduce_set(0, term_first, own_a, term_a, pair_a, sum_a, in_a, relay_a, acc_a)
-    reduce_set(1, term_second, own_b, term_b, pair_b, sum_b, in_b, relay_b, acc_b)
-
-    total = val_parts[dp].astype(wide)
-    for k in range(1, n_dp):
-        value_copies[k - 1].wait_recv()
-        total = total + val_landed[k].astype(wide)
-    piece = val_total.shape[1]
-    for c in range(n_ctx):
-        val_total[c] = total[c * piece : (c + 1) * piece]
-    value_pairs = []
-    for k in range(n_z):
-        dest = lax.rem(z + k, n_z)
-        val_term[k] = val_total[dest * 2 + other].astype(low)
-        copy = remote(val_term.at[k], val_pair.at[k], vp_send.at[k], vp_recv.at[k], partner)
-        copy.start()
-        value_pairs.append(copy)
-    pending.append((True, value_pairs))
+            for p in range(pieces):
+                key_stage[c, p * tokens : (p + 1) * tokens, :] = value[
+                    c * tokens : (c + 1) * tokens, p * lanes : (p + 1) * lanes
+                ]
+            key_stage[c, pieces * tokens :, :] = rope[:, c * tokens : (c + 1) * tokens]
+        own_k[at % slots] = key_stage[core]
+        term_k[at] = key_stage[other].astype(low)
+
+    def key_steps():
+        for at in range(n_z + lag):
+            if at < n_z:
+                key_terms(at)
+                key_set.begin(at, key_all, at)
+            if at >= lag:
+                key_set.finish(at - lag, key_all, at - lag)
+                key_set.push(0, at - lag)
+
+    def push_keys(p):
+        for at in range(n_z - 1):
+            key_set.push(p, at)
 
     def query_tile(i, carry):
-        if isinstance(i, int):
-            span = pl.ds(i * tile, tile)
-        else:
-            span = pl.ds(pl.multiple_of(i * tile, tile), tile)
+        span = pl.ds(pl.multiple_of(i * tile, tile), tile)
         piece = slope[:, span]
         all_lat = lat_all[...].reshape(n_ctx * tokens, latent)
         dql_ref[span, :] = dot(piece, all_lat, 0, 0).astype(low)
         qrf[span, :] = dot(piece, kr2[...], 0, 0)
         return carry
 
-    lax.fori_loop(0, rows // tile, query_tile, 0)
-    for at in range(heads // 2):
-        even = qrf[pl.ds(2 * at, tokens, stride=heads), :]
-        odd = qrf[pl.ds(2 * at + 1, tokens, stride=heads), :]
-        piece = jnp.where(lower, even, odd).T.astype(low)
-        dqr_ref[2 * at] = piece[:rope_width]
-        dqr_ref[2 * at + 1] = piece[rope_width:]
-
-    value_sends = []
-    for k in list(range(1, n_z)) + [0]:
-        value_pairs[k].wait_recv()
-        dest = lax.rem(z + k, n_z)
-        added = val_total[dest * 2 + core] + val_pair[k].astype(wide)
-        if k == 0:
-            uv_ref[...] = added
-        else:
-            val_sum[k] = added.astype(low)
-            copy = remote(val_sum.at[k], val_in.at[k], vz_send.at[k], vz_recv.at[k], chip_peer(dest))
-            copy.start()
-            value_sends.append(copy)
-    pending.append((True, value_sends))
-
-    def spread_dp(s, acc, msg, landing):
-        msg[...] = acc[...].astype(low)
-        landing[dp] = msg[...]
+    def query_terms(step):
+        count = rows // tile
+        middle = count // 2
+        lax.fori_loop(0 if step == 0 else middle, middle if step == 0 else count, query_tile, 0)
+        if step == 0:
+            return
+        for at in range(heads // 2):
+            even = qrf[pl.ds(2 * at, tokens, stride=heads), :]
+            odd = qrf[pl.ds(2 * at + 1, tokens, stride=heads), :]
+            piece = jnp.where(lower, even, odd).T.astype(low)
+            dqr_ref[2 * at] = piece[:rope_width]
+            dqr_ref[2 * at + 1] = piece[rope_width:]
+
+    shared = []
+
+    def spread_keys(p):
+        span = key_set.spans[p]
+        message[span] = acc_k[span].astype(low)
+        landed[dp, span] = message[span]
         copies = []
         for k in range(1, n_dp):
-            copy = remote(
-                msg, landing.at[dp], dp_send.at[s * n_dp + k], dp_recv.at[s * n_dp + k], dp_peer(k)
-            )
+            sem = p * n_dp + k
+            copy = remote(message.at[span], landed.at[dp, span], dp_send.at[sem], dp_recv.at[sem], dp_peer(k))
             copy.start()
             copies.append(copy)
         pending.append((True, copies))
-        return copies
-
-    collect(0, sum_a, in_a, acc_a)
-    first = spread_dp(0, acc_a, msg_a, blocks_a)
-    dlat_ref[:, :part] = msg_a[...]
-    collect(1, sum_b, in_b, acc_b)
-    second = spread_dp(1, acc_b, msg_b, blocks_b)
-    dlat_ref[:, part:] = msg_b[:tokens, :]
-    quarter = rope_width // 2
-    drope_ref[:quarter, :] = msg_b[tokens:, :tokens]
-    drope_ref[quarter:, :] = msg_b[tokens:, tokens:]
-
-    for copy in first:
-        copy.wait_recv()
-
-    def down_first(at, dest):
-        every = blocks_a[...].reshape(batch * tokens, part)
-        term_c[at] = dot(turned[dest * 2 + other], every, 1, 0).astype(low)
-        own_c[at % 2] = dot(turned[dest * 2 + core], every, 1, 0)
-
-    reduce_set(2, down_first, own_c, term_c, pair_c, sum_c, in_c, relay_c, acc_c)
-
-    for copy in second:
-        copy.wait_recv()
+        shared.append(copies)
+        dlat_ref[:, p * lanes : (p + 1) * lanes] = message[p * tokens : (p + 1) * tokens]
+        if p == pieces - 1:
+            drope_ref[...] = message[pieces * tokens :]
+
     packed = height % 32 == 0
-    for b in range(batch):
-        piece = blocks_b[b, tokens:, :]
-        cols = slice(b * tokens, (b + 1) * tokens)
-        for at in range(2):
-            rope_lo[at * quarter : (at + 1) * quarter, cols] = piece[:, at * tokens : (at + 1) * tokens]
-            rope_hi[rope_width + at * quarter : rope_width + (at + 1) * quarter, cols] = piece[
-                :, at * tokens : (at + 1) * tokens
-            ]
-    rope_lo[rope_width:, :] = jnp.zeros((rope_width, batch * tokens), low)
-    rope_hi[:rope_width, :] = jnp.zeros((rope_width, batch * tokens), low)
-
-    def down_piece(index):
-        every = blocks_b[:, :tokens, :].reshape(batch * tokens, part)
+    rope_rows = height // 2 if packed else padded
+    down_set = Reduce(
+        spans_of(padded, rope_rows), own_d, term_d, pair_d, sum_d, in_d, relay_d, acc_d,
+        (gp_send, gp_recv, gz_send, gz_recv, gr_recv),
+    )
+
+    def down_piece(p, index):
+        every = landed[:, p * tokens : (p + 1) * tokens, :].reshape(batch * tokens, lanes)
         lat = dot(turned[index], every, 1, 0)
+        if p < pieces - 1:
+            return lat
         if packed:
             rope = dot(turned[index, : height // 2], rope_lo[...], 1, 1)
             rope = rope + dot(turned[index, height // 2 :], rope_hi[...], 1, 1)
-            rope = jnp.concatenate([rope[: height // 4], rope[height // 4 :]], axis=1)
         else:
             rope = dot(turned[index], rope_lo[...], 1, 1)
-            rope = jnp.concatenate([rope, jnp.zeros((padded, part - two), wide)], axis=1)
-        return lat, rope
-
-    def down_second(at, dest):
-        lat, rope = down_piece(dest * 2 + other)
-        term_d[at, :padded, :] = lat.astype(low)
-        term_d[at, padded:, :] = rope.astype(low)
-        lat, rope = down_piece(dest * 2 + core)
-        own_d[at % 2, :padded, :] = lat
-        own_d[at % 2, padded:, :] = rope
-
-    reduce_set(3, down_second, own_d, term_d, pair_d, sum_d, in_d, relay_d, acc_d)
+        return jnp.concatenate([lat, rope], axis=0)
+
+    def down_terms(p):
+        for copy in shared[p]:
+            copy.wait_recv()
+        if p == pieces - 1:
+            for b in range(batch):
+                piece = landed[b, pieces * tokens :, :]
+                cols = slice(b * tokens, (b + 1) * tokens)
+                rope_lo[:rope_width, cols] = piece
+                rope_hi[rope_width:, cols] = piece
+            rope_lo[rope_width:, :] = jnp.zeros((rope_width, batch * tokens), low)
+            rope_hi[:rope_width, :] = jnp.zeros((rope_width, batch * tokens), low)
+        span = down_set.spans[p]
+        for at in range(n_z + lag):
+            if at < n_z:
+                dest = down_set.dest(at)
+                term_d[at, span] = down_piece(p, dest * 2 + other).astype(low)
+                down_set.begin(at, span, p * n_z + at)
+                own_d[at % slots, span] = down_piece(p, dest * 2 + core)
+            if at >= lag:
+                down_set.finish(at - lag, span, p * n_z + at - lag)
+                down_set.push(p, at - lag)
+
+    key_steps()
+    push_keys(1)
+    key_set.relay(0)
+    push_keys(2)
+    query_terms(0)
+    key_set.relay(1)
+    push_keys(3)
+    key_set.collect(0)
+    spread_keys(0)
+    pair_values()
+    key_set.relay(2)
+    key_set.collect(1)
+    spread_keys(1)
+    query_terms(1)
+    start_values()
+    key_set.relay(3)
+    down_terms(0)
+    key_set.collect(2)
+    spread_keys(2)
+    key_set.collect(3)
+    spread_keys(3)
+    down_terms(1)
+    down_set.relay(0)
+    down_terms(2)
+    down_set.relay(1)
+    down_terms(3)
+    down_set.relay(2)
+    down_set.relay(3)
     for k in range(1, n_z):
         value_sends[k - 1].wait_recv()
         uv_ref[...] += val_in[k].astype(wide)
-    collect(2, sum_c, in_c, acc_c)
-    down_ref[:, :part] = acc_c[:height, :]
-    collect(3, sum_d, in_d, acc_d)
-    down_ref[:, part:latent] = acc_d[:height, :]
+    for p in range(pieces):
+        down_set.collect(p)
+        down_ref[:, p * lanes : (p + 1) * lanes] = acc_d[p * padded : p * padded + height]
+    rope = acc_d[pieces * padded :]
     if packed:
-        rope = acc_d[padded:, :]
-        rope = jnp.concatenate([rope[:, :two], rope[:, two:]], axis=0)
         down_ref[: height // 2, latent:] = rope[:, :rope_width]
         down_ref[height // 2 :, latent:] = rope[:, rope_width:]
     else:
-        down_ref[:, latent:] = acc_d[padded : padded + height, :rope_width]
+        down_ref[:, latent:] = rope[:height, :rope_width]
 
     for ok, copies in pending:
         when(ok, functools.partial(send_waits, copies))
@@ -556,21 +611,21 @@
     batch, _, width = layer_input.shape
     height = width // n_ctx
     padded = -(-height // 16) * 16
-    extra = height // 4 if height % 32 == 0 else padded
+    down_fill = 4 * padded + (height // 2 if height % 32 == 0 else padded)
+    key_fill = 4 * tokens + rope_width
+    pieces = 4
     share = latent // (n_dp * n_ctx)
-    part = latent // 2
     two = 2 * rope_width
     vmem = pl.BlockSpec(memory_space=pltpu.VMEM)
     hbm = pl.BlockSpec(memory_space=pltpu.HBM)
     dma = lambda n: pltpu.SemaphoreType.DMA((n,))
 
-    def stage(count, fill, landed):
-        half = lambda *dims: pltpu.VMEM((*dims, fill, part), low)
-        out = [
-            pltpu.VMEM((count, fill, part), wide), half(n_z), half(n_z), half(n_z), half(n_z), half(),
-            pltpu.VMEM((fill, part), wide),
+    def stage(fill):
+        half = lambda *dims: pltpu.VMEM((*dims, fill, 128), low)
+        return [
+            pltpu.VMEM((4, fill, 128), wide), half(n_z), half(n_z), half(n_z), half(n_z), half(),
+            pltpu.VMEM((fill, 128), wide),
         ]
-        return out + ([half(), half(batch)] if landed else [])
 
     outs = (
         ((rows, latent), low),
@@ -615,15 +670,18 @@
             pltpu.VMEM((n_z, share, values), low),
             pltpu.VMEM((n_z, share, values), low),
             pltpu.VMEM((n_z, share, values), low),
-            *stage(4, tokens, True),
-            *stage(4, tokens + rope_width // 2, True),
-            *stage(2, padded, False),
-            *stage(2, padded + extra, False),
+            pltpu.VMEM((2, key_fill, 128), wide),
+            *stage(key_fill),
+            pltpu.VMEM((key_fill, 128), low),
+            pltpu.VMEM((n_dp, key_fill, 128), low),
+            *stage(down_fill),
             pltpu.VMEM((two, batch * tokens), low),
             pltpu.VMEM((two, batch * tokens), low),
-            dma(8), dma(2 * n_z), dma(2 * n_z), dma(2 * n_z), dma(2 * n_z), dma(2),
+            dma(8), dma(3 * n_z), dma(3 * n_z), dma(3 * n_z), dma(3 * n_z), dma(3 * n_z),
             dma(n_dp), dma(n_dp), dma(n_z), dma(n_z), dma(n_z), dma(n_z),
-            dma(4 * n_z), dma(4 * n_z), dma(4 * n_z), dma(4 * n_z), dma(4), dma(2 * n_dp), dma(2 * n_dp),
+            dma(n_z), dma(n_z), dma(pieces * n_z), dma(pieces * n_z), dma(pieces),
+            dma(pieces * n_z), dma(pieces * n_z), dma(pieces * n_z), dma(pieces * n_z), dma(pieces),
+            dma(pieces * n_dp), dma(pieces * n_dp),
         ],
         compiler_params=pltpu.CompilerParams(
             collective_id=0, has_side_effects=True, vmem_limit_bytes=VMEM_LIMIT

time: 68.6 us -> 60.6 us (0.88); the launches traced: 67.6 us -> 60.5 us
  Pallas kernels: 66.8 us -> 59.7 us
    pallas_call x1, Pallas kernels: 65.5 us -> 58.4 us  [body(): pl.pallas_call(functools.partial(main_kernel, n_dp, n_ctx), out_shape=tup...]
where the time goes in v2:
time: 60.6 us; the launch traced here: 60.5 us
  Pallas kernels  59.7 us (99%)
  between operations  0.8 us (1%)
    pallas_call x1, Pallas kernels, body(): pl.pallas_call(functools.partial(main_kernel, n_dp, n_ctx), out_shape=tup...  58.4 us
    pallas_call x1, Pallas kernels, body(): pl.pallas_call(functools.partial(store_kernel, len(outs)), out_shape=tupl...  1.31 us

profile of v2, /device:TPU:0, one launch (start us, length us, event | category | flops | bytes accessed | tf_op | source)
XLA Modules:
  0.0 60.5 jit_solution(5468929808147044313)
XLA Ops:
  0.6 58.4 %main.1 = (bf16[1024,512]{1,0:T(8,128)(2,1)S(1)}, bf16[8,64,128]{2,1,0:T(8,128)(2,1)S(1)}, bf16[128,512]{1,0:T(8,128)(2,1)S(1)}, bf16[64,128]{1,0:T(8,128)(2,1)S...) custom-call(s32[16]{0:T(128)} %blocks_ref.1, bf16[128,512]{1,0:T(8,128)(2,1)} %bitcast.21, bf16[64,128]{1,0:T(8,128)(2,1)} %bitcast.23, ...), custom_call_target="tpu_custom_call" | custom-call | tf_op jit(solution)/shard_map/main/pallas_call | solution.py:638
  59.0 1.3 %store.1 = (bf16[1024,512]{1,0:T(8,128)(2,1)}, bf16[8,64,128]{2,1,0:T(8,128)(2,1)}, bf16[128,512]{1,0:T(8,128)(2,1)}, bf16[64,128]{1,0:T(8,128)(2,1)}, f32[224,576]{1,0:T(8,128)}, /*index=5*/f32[16,1024]{1,0:T(8,128)}) custom-call(bf16[1024,512]{1,0:T(8,128)(2,1)S(1)} %get-tuple-element.18.refs_0_, bf16[8,64,128]{2,1,0:T(8,128)(2,1)S(1)} %get-tuple-element.19.refs_1_, ...), custom_call_target="tpu_custom_call" | custom-call | tf_op jit(solution)/shard_map/store/pallas_call | solution.py:695

commit v3 on v2

--- a/solution.py
+++ b/solution.py
@@ -93,7 +93,7 @@
     lat_all, rope_all, kr2, ql, qrt, qrf, qr2, qr2t, saved, weight, dout, layer, turned,
     spread, grad, delta, posk, expo, slope, tops, sums, factor,
     val_parts, val_landed, val_total, val_term, val_pair, val_sum, val_in,
-    key_stage, own_k, term_k, pair_k, sum_k, in_k, relay_k, acc_k, message, landed,
+    key_stage, own_k, term_k, landing_k, sum_k, in_k, relay_k, acc_k, message, landed,
     own_d, term_d, pair_d, sum_d, in_d, relay_d, acc_d,
     rope_lo, rope_hi,
     local_sem, key_send, key_recv, fwd_send, fwd_recv, relay_send,
@@ -117,7 +117,6 @@
     values = dout.shape[1]
     pieces = 4
     lanes = latent // pieces
-    pending = []
 
     def local(at, src, dst):
         copy = pltpu.make_async_copy(src, dst, local_sem.at[at])
@@ -145,31 +144,31 @@
     rope_in.wait()
     pl.semaphore_wait(barrier, len(peers))
 
-    def key_copies(owner, sends, recvs, send_at, recv_at, peer):
+    def key_copies(owner, sends, recvs, recv_at, peer):
         index = owner * 2 + core
         refs = [lat_all.at[index, pl.ds(0, half)], lat_all.at[index, pl.ds(half, half)], rope_all.at[index]]
         return [
-            remote(ref, ref, sends.at[n * n_z + send_at], recvs.at[n * n_z + recv_at], peer)
-            for n, ref in enumerate(refs)
+            remote(ref, ref, sends.at[n // 2], recvs.at[recv_at[n]], peer) for n, ref in enumerate(refs)
         ]
+
+    def apart(owner):
+        return [n * n_z + owner for n in range(3)]
+
+    def key_blocks_sent(sends, count):
+        for n, ref in enumerate([lat_all, rope_all]):
+            blocks = ref.at[pl.ds(0, count)]
+            remote(blocks, blocks, sends.at[n], key_recv.at[0], partner).wait_send()
 
     def start_all(copies):
         for copy in copies:
             copy.start()
 
-    def send_waits(copies):
-        for copy in copies:
-            copy.wait_send()
-
     for at in range(n_z - 1):
         dest = pick(z, line.column(line.gather, at))
         ok = flag(z, [not line.ends(c, line.gather[c][at]) for c in range(n_z)])
-        copies = key_copies(z, key_send, key_recv, at, z, chip_peer(dest))
+        copies = key_copies(z, key_send, key_recv, apart(z), chip_peer(dest))
         when(ok, functools.partial(start_all, copies))
-        pending.append((ok, copies))
-    copies = key_copies(z, fwd_send, fwd_recv, z, z, partner)
-    start_all(copies)
-    pending.append((True, copies))
+    start_all(key_copies(z, fwd_send, fwd_recv, [z] * 3, partner))
 
     out_in.wait()
     lane = lax.broadcasted_iota(jnp.int32, (heads, values), 1)
@@ -200,11 +199,10 @@
     value_copies = []
     for k in range(1, n_dp):
         copy = remote(
-            val_parts.at[lax.rem(dp + k, n_dp)], val_landed.at[k], val_send.at[k], val_recv.at[k], dp_peer(k)
+            val_parts.at[lax.rem(dp + k, n_dp)], val_landed.at[k], val_send.at[0], val_recv.at[0], dp_peer(k)
         )
         copy.start()
         value_copies.append(copy)
-    pending.append((True, value_copies))
 
     weight_in.wait()
     tile = min(256, rows)
@@ -221,13 +219,10 @@
     low_block, high_block = blocks_ref[2 * ctx], blocks_ref[2 * ctx + 1]
 
     def pass_on(owner):
-        copies = key_copies(owner, fwd_send, fwd_recv, owner, owner, partner)
-        start_all(copies)
-        pending.append((True, copies))
+        start_all(key_copies(owner, fwd_send, fwd_recv, [owner] * 3, partner))
 
     def chunk(owner):
-        for copy in key_copies(owner, fwd_send, fwd_recv, 0, owner, partner):
-            copy.wait_recv()
+        remote(term_k.at[0], landing_k.at[0], fwd_send.at[0], fwd_recv.at[owner], partner).wait_recv()
         keys = pl.ds(pl.multiple_of(owner * chip_rows, chip_rows), chip_rows)
         for at in range(2):
             piece = rope_all[owner * 2 + at].astype(wide)
@@ -281,9 +276,10 @@
     value_pairs, value_sends = [], []
 
     def pair_values():
+        others = pl.ds(1, n_dp - 1)
+        remote(val_parts.at[others], val_landed.at[others], val_send.at[0], val_recv.at[0], partner).wait_recv()
         total = val_parts[dp].astype(wide)
         for k in range(1, n_dp):
-            value_copies[k - 1].wait_recv()
             total = total + val_landed[k].astype(wide)
         piece = val_total.shape[1]
         for c in range(n_ctx):
@@ -291,24 +287,22 @@
         for k in range(n_z):
             dest = lax.rem(z + k, n_z)
             val_term[k] = val_total[dest * 2 + other].astype(low)
-            copy = remote(val_term.at[k], val_pair.at[k], vp_send.at[k], vp_recv.at[k], partner)
+            copy = remote(val_term.at[k], val_pair.at[k], vp_send.at[0], vp_recv.at[0], partner)
             copy.start()
             value_pairs.append(copy)
-        pending.append((True, value_pairs))
 
     def start_values():
+        remote(val_term, val_pair, vp_send.at[0], vp_recv.at[0], partner).wait_recv()
         for k in list(range(1, n_z)) + [0]:
-            value_pairs[k].wait_recv()
             dest = lax.rem(z + k, n_z)
             added = val_total[dest * 2 + core] + val_pair[k].astype(wide)
             if k == 0:
                 uv_ref[...] = added
             else:
                 val_sum[k] = added.astype(low)
-                copy = remote(val_sum.at[k], val_in.at[k], vz_send.at[k], vz_recv.at[k], chip_peer(dest))
+                copy = remote(val_sum.at[k], val_in.at[k], vz_send.at[0], vz_recv.at[0], chip_peer(dest))
                 copy.start()
                 value_sends.append(copy)
-        pending.append((True, value_sends))
 
     for at in range(n_z - 1):
         owner = pick(z, line.column(line.arrive, at))
@@ -316,9 +310,8 @@
         copies = []
         if relay_ok is not False:
             end = jnp.where(z == 1, 0, n_z - 1)
-            copies = key_copies(owner, relay_send, key_recv, 0, owner, chip_peer(end))
-            pending.append((relay_ok, copies))
-        for n, copy in enumerate(key_copies(owner, key_send, key_recv, 0, owner, partner)):
+            copies = key_copies(owner, relay_send, key_recv, apart(owner), chip_peer(end))
+        for n, copy in enumerate(key_copies(owner, key_send, key_recv, apart(owner), partner)):
             copy.wait_recv()
             if copies:
                 when(relay_ok, copies[n].start)
@@ -341,6 +334,7 @@
 
     lag, slots = 2, 4
     neighbour = jnp.where(z == 0, 1, n_z - 2)
+    at_end = flag(z, [line.hybrid and c in (0, n_z - 1) for c in range(n_z)])
 
     class Reduce:
         def __init__(self, spans, own, term, landing, total, inbox, relay, acc, sems):
@@ -354,21 +348,19 @@
 
         def pair(self, at, span, sem):
             return remote(
-                self.term.at[at, span], self.landing.at[at, span], self.pair_send.at[sem], self.pair_recv.at[sem], partner
+                self.term.at[at, span], self.landing.at[at, span], self.pair_send.at[0], self.pair_recv.at[sem], partner
             )
 
-        def straight(self, p, at, source=None):
-            sem = p * n_z
-            source = z if source is None else source
+        def straight(self, p, at):
             return remote(
-                self.total.at[at, self.spans[p]], self.inbox.at[source, self.spans[p]],
-                self.send.at[sem + at], self.recv.at[sem + source], chip_peer(self.dest(at)),
+                self.total.at[at, self.spans[p]], self.inbox.at[z, self.spans[p]],
+                self.send.at[0], self.recv.at[p], chip_peer(self.dest(at)),
             )
 
         def aside(self, p, at):
             return remote(
                 self.total.at[at, self.spans[p]], self.relayed.at[self.spans[p]],
-                self.send.at[p * n_z + at], self.relay_recv.at[p], chip_peer(neighbour),
+                self.send.at[0], self.relay_recv.at[p], chip_peer(neighbour),
             )
 
         def consumer(self, at):
@@ -378,9 +370,7 @@
             return self.own[at % slots, span] + self.landing[at, span].astype(wide)
 
         def begin(self, at, span, sem):
-            copy = self.pair(at, span, sem)
-            copy.start()
-            pending.append((True, [copy]))
+            self.pair(at, span, sem).start()
 
         def finish(self, at, span, sem):
             self.pair(at, span, sem).wait_recv()
@@ -400,7 +390,6 @@
                 otherwise(origin, self.straight(p, at).start)
 
             otherwise(self.consumer(at), out)
-            pending.append((True, [self.straight(p, at)]))
 
         def relay(self, p):
             span = self.spans[p]
@@ -415,15 +404,31 @@
 
         def collect(self, p):
             span = self.spans[p]
+
+            def arrived(count):
+                blocks = pl.ds(0, count)
+                remote(
+                    self.total.at[blocks, span], self.inbox.at[blocks, span],
+                    self.send.at[0], self.recv.at[p], partner,
+                ).wait_recv()
+
+            when(at_end, functools.partial(arrived, n_z - 2))
+            otherwise(at_end, functools.partial(arrived, n_z - 1))
             for at in range(n_z - 1):
                 source = pick(z, line.column(line.near, at))
                 ok = flag(z, [not line.ends(c, line.near[c][at]) for c in range(n_z)])
 
                 def add():
-                    self.straight(p, 0, source).wait_recv()
                     self.acc[span] += self.inbox[source, span].astype(wide)
 
                 when(ok, add)
+
+        def sent(self):
+            blocks = pl.ds(0, n_z - 1)
+            remote(self.term, self.landing, self.pair_send.at[0], self.pair_recv.at[0], partner).wait_send()
+            remote(
+                self.total.at[blocks], self.inbox.at[blocks], self.send.at[0], self.recv.at[0], partner
+            ).wait_send()
 
     def spans_of(size, tail):
         return [pl.ds(p * size, size + (tail if p == pieces - 1 else 0)) for p in range(pieces)]
@@ -431,7 +436,7 @@
     key_fill = pieces * tokens + rope_width
     key_all = pl.ds(0, key_fill)
     key_set = Reduce(
-        spans_of(tokens, rope_width), own_k, term_k, pair_k, sum_k, in_k, relay_k, acc_k,
+        spans_of(tokens, rope_width), own_k, term_k, landing_k, sum_k, in_k, relay_k, acc_k,
         (kp_send, kp_recv, kz_send, kz_recv, kr_recv),
     )
 
@@ -454,13 +459,13 @@
         term_k[at] = key_stage[other].astype(low)
 
     def key_steps():
-        for at in range(n_z + lag):
+        for at in range(n_z + 1):
             if at < n_z:
                 key_terms(at)
                 key_set.begin(at, key_all, at)
-            if at >= lag:
-                key_set.finish(at - lag, key_all, at - lag)
-                key_set.push(0, at - lag)
+            if at >= 1:
+                key_set.finish(at - 1, key_all, at - 1)
+                key_set.push(0, at - 1)
 
     def push_keys(p):
         for at in range(n_z - 1):
@@ -487,20 +492,14 @@
             dqr_ref[2 * at] = piece[:rope_width]
             dqr_ref[2 * at + 1] = piece[rope_width:]
 
-    shared = []
-
     def spread_keys(p):
         span = key_set.spans[p]
         message[span] = acc_k[span].astype(low)
         landed[dp, span] = message[span]
-        copies = []
         for k in range(1, n_dp):
-            sem = p * n_dp + k
-            copy = remote(message.at[span], landed.at[dp, span], dp_send.at[sem], dp_recv.at[sem], dp_peer(k))
-            copy.start()
-            copies.append(copy)
-        pending.append((True, copies))
-        shared.append(copies)
+            remote(
+                message.at[span], landed.at[dp, span], dp_send.at[0], dp_recv.at[p], dp_peer(k)
+            ).start()
         dlat_ref[:, p * lanes : (p + 1) * lanes] = message[p * tokens : (p + 1) * tokens]
         if p == pieces - 1:
             drope_ref[...] = message[pieces * tokens :]
@@ -525,8 +524,9 @@
         return jnp.concatenate([lat, rope], axis=0)
 
     def down_terms(p):
-        for copy in shared[p]:
-            copy.wait_recv()
+        others = pl.ds(0, n_dp - 1)
+        arrived = landed.at[others, key_set.spans[p]]
+        remote(arrived, arrived, dp_send.at[0], dp_recv.at[p], partner).wait_recv()
         if p == pieces - 1:
             for b in range(batch):
                 piece = landed[b, pieces * tokens :, :]
@@ -574,8 +574,9 @@
     down_terms(3)
     down_set.relay(2)
     down_set.relay(3)
+    others = pl.ds(1, n_z - 1)
+    remote(val_sum.at[others], val_in.at[others], vz_send.at[0], vz_recv.at[0], partner).wait_recv()
     for k in range(1, n_z):
-        value_sends[k - 1].wait_recv()
         uv_ref[...] += val_in[k].astype(wide)
     for p in range(pieces):
         down_set.collect(p)
@@ -587,13 +588,31 @@
     else:
         down_ref[:, latent:] = rope[:height, :rope_width]
 
-    for ok, copies in pending:
-        when(ok, functools.partial(send_waits, copies))
+    when(at_end, functools.partial(key_blocks_sent, key_send, n_z - 2))
+    otherwise(at_end, functools.partial(key_blocks_sent, key_send, n_z - 1))
+    key_blocks_sent(fwd_send, n_z)
+    relays = flag(z, [line.hybrid and c in (1, n_z - 2) for c in range(n_z)])
+    when(relays, functools.partial(key_blocks_sent, relay_send, 1))
+    others = pl.ds(0, n_dp - 1)
+    remote(val_parts.at[others], val_landed.at[others], val_send.at[0], val_recv.at[0], partner).wait_send()
+    remote(val_term, val_pair, vp_send.at[0], vp_recv.at[0], partner).wait_send()
+    others = pl.ds(0, n_z - 1)
+    remote(val_sum.at[others], val_in.at[others], vz_send.at[0], vz_recv.at[0], partner).wait_send()
+    key_set.sent()
+    down_set.sent()
+    sent = landed.at[pl.ds(0, n_dp - 1)]
+    remote(sent, sent, dp_send.at[0], dp_recv.at[0], partner).wait_send()
 
 
 def store_kernel(n, *refs):
     sem = refs[2 * n]
-    copies = [pltpu.make_async_copy(refs[at], refs[n + at], sem.at[at]) for at in range(n)]
+    copies = []
+    for at in range(n):
+        rows = refs[at].shape[0]
+        parts = 4 if rows % 64 == 0 and rows >= 512 else 1
+        for part in range(parts):
+            span = pl.ds(part * (rows // parts), rows // parts)
+            copies.append(pltpu.make_async_copy(refs[at].at[span], refs[n + at].at[span], sem.at[len(copies)]))
     for copy in copies:
         copy.start()
     for copy in copies:
@@ -677,11 +696,11 @@
             *stage(down_fill),
             pltpu.VMEM((two, batch * tokens), low),
             pltpu.VMEM((two, batch * tokens), low),
-            dma(8), dma(3 * n_z), dma(3 * n_z), dma(3 * n_z), dma(3 * n_z), dma(3 * n_z),
-            dma(n_dp), dma(n_dp), dma(n_z), dma(n_z), dma(n_z), dma(n_z),
-            dma(n_z), dma(n_z), dma(pieces * n_z), dma(pieces * n_z), dma(pieces),
-            dma(pieces * n_z), dma(pieces * n_z), dma(pieces * n_z), dma(pieces * n_z), dma(pieces),
-            dma(pieces * n_dp), dma(pieces * n_dp),
+            dma(8), dma(2), dma(3 * n_z), dma(2), dma(n_z), dma(2),
+            dma(1), dma(1), dma(1), dma(1), dma(1), dma(1),
+            dma(1), dma(n_z), dma(1), dma(pieces), dma(pieces),
+            dma(1), dma(pieces * n_z), dma(1), dma(pieces), dma(pieces),
+            dma(1), dma(pieces),
         ],
         compiler_params=pltpu.CompilerParams(
             collective_id=0, has_side_effects=True, vmem_limit_bytes=VMEM_LIMIT
@@ -697,7 +716,7 @@
         out_shape=tuple(jax.ShapeDtypeStruct(shape, kind) for shape, kind in outs),
         in_specs=[vmem] * len(outs),
         out_specs=(hbm,) * len(outs),
-        scratch_shapes=[dma(len(outs))],
+        scratch_shapes=[dma(len(outs) + 3)],
         compiler_params=pltpu.CompilerParams(vmem_limit_bytes=4 * 1024 * 1024),
         name="store",
     )(*found)

time: 60.6 us -> 59.6 us (0.983)
  Pallas kernels: 59.7 us -> 58.7 us
    pallas_call x1, Pallas kernels: 58.4 us -> 57.3 us  [body(): pl.pallas_call(functools.partial(main_kernel, n_dp, n_ctx), out_shape=tup...]
where the time goes in v3:
time: 59.6 us; the launch traced here: 59.5 us
  Pallas kernels  58.7 us (98%)
  between operations  0.8 us (1%)
    pallas_call x1, Pallas kernels, body(): pl.pallas_call(functools.partial(main_kernel, n_dp, n_ctx), out_shape=tup...  57.3 us
    pallas_call x1, Pallas kernels, body(): pl.pallas_call(functools.partial(store_kernel, len(outs)), out_shape=tupl...  1.34 us

profile of v3, /device:TPU:0, one launch (start us, length us, event | category | flops | bytes accessed | tf_op | source)
XLA Modules:
  0.0 59.5 jit_solution(11398791687218769586)
XLA Ops:
  0.6 57.3 %main.1 = (bf16[1024,512]{1,0:T(8,128)(2,1)S(1)}, bf16[8,64,128]{2,1,0:T(8,128)(2,1)S(1)}, bf16[128,512]{1,0:T(8,128)(2,1)S(1)}, bf16[64,128]{1,0:T(8,128)(2,1)S...) custom-call(s32[16]{0:T(128)} %blocks_ref.1, bf16[128,512]{1,0:T(8,128)(2,1)} %bitcast.21, bf16[64,128]{1,0:T(8,128)(2,1)} %bitcast.23, ...), custom_call_target="tpu_custom_call" | custom-call | tf_op jit(solution)/shard_map/main/pallas_call | solution.py:657
  58.0 1.3 %store.1 = (bf16[1024,512]{1,0:T(8,128)(2,1)}, bf16[8,64,128]{2,1,0:T(8,128)(2,1)}, bf16[128,512]{1,0:T(8,128)(2,1)}, bf16[64,128]{1,0:T(8,128)(2,1)}, f32[224,576]{1,0:T(8,128)}, /*index=5*/f32[16,1024]{1,0:T(8,128)}) custom-call(bf16[1024,512]{1,0:T(8,128)(2,1)S(1)} %get-tuple-element.18.refs_0_, bf16[8,64,128]{2,1,0:T(8,128)(2,1)S(1)} %get-tuple-element.19.refs_1_, ...), custom_call_target="tpu_custom_call" | custom-call | tf_op jit(solution)/shard_map/store/pallas_call | solution.py:714

commit v4 on v3

--- a/solution.py
+++ b/solution.py
@@ -459,13 +459,13 @@
         term_k[at] = key_stage[other].astype(low)
 
     def key_steps():
-        for at in range(n_z + 1):
+        for at in range(n_z + lag):
             if at < n_z:
                 key_terms(at)
                 key_set.begin(at, key_all, at)
-            if at >= 1:
-                key_set.finish(at - 1, key_all, at - 1)
-                key_set.push(0, at - 1)
+            if at >= lag:
+                key_set.finish(at - lag, key_all, at - lag)
+                key_set.push(0, at - lag)
 
     def push_keys(p):
         for at in range(n_z - 1):
@@ -560,14 +560,14 @@
     key_set.collect(1)
     spread_keys(1)
     query_terms(1)
+    key_set.relay(3)
     start_values()
-    key_set.relay(3)
     down_terms(0)
     key_set.collect(2)
     spread_keys(2)
+    down_terms(1)
     key_set.collect(3)
     spread_keys(3)
-    down_terms(1)
     down_set.relay(0)
     down_terms(2)
     down_set.relay(1)

time: 59.6 us -> 59.2 us (level)
  no operation moved by 1% of the time
where the time goes in v4:
time: 59.2 us; the launch traced here: 59.1 us
  Pallas kernels  58.3 us (98%)
  between operations  0.8 us (1%)
    pallas_call x1, Pallas kernels, body(): pl.pallas_call(functools.partial(main_kernel, n_dp, n_ctx), out_shape=tup...  56.9 us
    pallas_call x1, Pallas kernels, body(): pl.pallas_call(functools.partial(store_kernel, len(outs)), out_shape=tupl...  1.34 us

profile of v4, /device:TPU:0, one launch (start us, length us, event | category | flops | bytes accessed | tf_op | source)
XLA Modules:
  0.0 59.1 jit_solution(17625622230784420931)
XLA Ops:
  0.6 56.9 %main.1 = (bf16[1024,512]{1,0:T(8,128)(2,1)S(1)}, bf16[8,64,128]{2,1,0:T(8,128)(2,1)S(1)}, bf16[128,512]{1,0:T(8,128)(2,1)S(1)}, bf16[64,128]{1,0:T(8,128)(2,1)S...) custom-call(s32[16]{0:T(128)} %blocks_ref.1, bf16[128,512]{1,0:T(8,128)(2,1)} %bitcast.21, bf16[64,128]{1,0:T(8,128)(2,1)} %bitcast.23, ...), custom_call_target="tpu_custom_call" | custom-call | tf_op jit(solution)/shard_map/main/pallas_call | solution.py:657
  57.6 1.3 %store.1 = (bf16[1024,512]{1,0:T(8,128)(2,1)}, bf16[8,64,128]{2,1,0:T(8,128)(2,1)}, bf16[128,512]{1,0:T(8,128)(2,1)}, bf16[64,128]{1,0:T(8,128)(2,1)}, f32[224,576]{1,0:T(8,128)}, /*index=5*/f32[16,1024]{1,0:T(8,128)}) custom-call(bf16[1024,512]{1,0:T(8,128)(2,1)S(1)} %get-tuple-element.18.refs_0_, bf16[8,64,128]{2,1,0:T(8,128)(2,1)S(1)} %get-tuple-element.19.refs_1_, ...), custom_call_target="tpu_custom_call" | custom-call | tf_op jit(solution)/shard_map/store/pallas_call | solution.py:714
